TPU v7x, 256 devices: a whole 4x4x8 slice. The times are simulated.
256 devices in a mesh: robot: 16 (over y, x_lo, core), seed: 16 (over x_hi, z).
Axes of the slice: x: 4 (x_hi: 2, x_lo: 2; x = x_hi * 2 + x_lo), y: 4, z: 8, core: 2. Of those that a mesh axis runs over, the one named last changes fastest.
Arguments:
- centres: float32 [32, 3, 52, 4096], P('robot', None, None, 'seed'), may hold values from -52 to 52
- sphere_radius: float32 [32, 52], P('robot'), may hold values from 0.2 to 0.8
- counts: int32 [32], P('robot'), may hold values from 26 to 52
- adjacency: int32 [32, 32], P('robot'), may hold values from 0 to 1, as said below
Outputs:
- collision_cost: float32 [32, 4096], P('robot', 'seed')
- blended_path: float32 [32, 3, 52, 32], P('robot')
Inputs may be any that keep to these rules, and one draw needn't show every extreme that they name: `adjacency`: symmetric, with zeros on the diagonal.
All inputs are finite; a program needn't handle non-finite values.
Results may differ from a plain program's by a relative error of at most 0.0003.
Values sent between devices are 32-bit elements; how exact they have to be, the bound alone decides.
A program may use at most 64 MiB of HBM per device.

v0:
```python
import jax
import jax.numpy as jnp
from jax import lax
from jax.sharding import PartitionSpec as P

W = 32


lane_width = 128


def shifted(block, axis, distance):
    devices = range(lax.axis_size(axis))
    route = [((i - distance) % len(devices), i) for i in devices]
    return lax.ppermute(block, axis, route)


def sent_to_all(array, axis):
    copies = jnp.broadcast_to(array, (lax.axis_size(axis), *array.shape))
    return lax.all_to_all(copies, axis, split_axis=0, concat_axis=0, tiled=True)


def over_copies(array, axis):
    everything = sent_to_all(array, axis)
    return jnp.sum(everything, axis=0)


def in_one(arrays, axis):
    ends = [0]
    for a in arrays:
        ends.append(ends[-1] + a.size)
    so_far = over_copies(jnp.concatenate([a.ravel() for a in arrays]), axis)
    return tuple((so_far[b:e].reshape(a.shape) for a, b, e in zip(arrays, ends, ends[1:])))


def swept_blocks(centres, sphere_radius):
    robots_here, _, spheres, columns = centres.shape
    shaped = centres.reshape(robots_here, 3, spheres, columns // W, W)
    ahead_point = jnp.concatenate([shaped[..., 1:], shaped[..., -1:]], axis=4)
    middle = 0.5 * (shaped + ahead_point)
    step_length = jnp.sqrt(jnp.sum((ahead_point - shaped) ** 2, axis=1) + 1e-06)
    swept_radius = sphere_radius[:, :, None, None] + 0.5 * step_length
    swept_block = jnp.concatenate([middle, swept_radius[:, None]], axis=1)
    return swept_block.reshape(robots_here, 4, spheres, columns)


def active_spheres(counts, spheres):
    return (jnp.arange(spheres, dtype=jnp.int32)[None, :] < counts[:, None]).astype(jnp.float32)


def pair_cost(first_block, first_active, second_block, second_active, sphere_mask):
    spheres = first_block.shape[1]
    columns = first_block.shape[2]
    weights = first_active[:, None] * second_active[None, :] * sphere_mask

    def tile_cost(tile_index):
        offset = tile_index * lane_width
        first_tile = lax.dynamic_slice_in_dim(first_block, offset, lane_width, 2)
        second_tile = lax.dynamic_slice_in_dim(second_block, offset, lane_width, 2)
        distance = jnp.zeros((spheres, spheres, lane_width), jnp.float32)
        for axis_index in range(3):
            gap = first_tile[axis_index][:, None, :] - second_tile[axis_index][None, :, :]
            distance = distance + gap * gap
        spread = first_tile[3][:, None, :] + second_tile[3][None, :, :]
        return jnp.sum(weights[:, :, None] * jnp.exp(-distance / (spread * spread)), axis=(0, 1))

    tiles = lax.map(tile_cost, jnp.arange(columns // lane_width, dtype=jnp.int32))
    return tiles.reshape(columns) / (spheres * spheres)


def self_costs(own_blocks, own_active):
    spheres = own_blocks.shape[2]
    order = jnp.arange(spheres, dtype=jnp.int32)
    apart = (order[None, :] >= order[:, None] + 2).astype(jnp.float32)

    def single(robot_row):
        return pair_cost(
            own_blocks[robot_row],
            own_active[robot_row],
            own_blocks[robot_row],
            own_active[robot_row],
            apart,
        )

    return lax.map(single, jnp.arange(own_blocks.shape[0], dtype=jnp.int32))


def cross_costs(own_blocks, own_active, other_blocks, other_active, link_rows):
    robots_here = own_blocks.shape[0]
    arrived_count = other_blocks.shape[0]
    spheres = own_blocks.shape[2]
    columns = own_blocks.shape[3]
    full_mask = jnp.ones((spheres, spheres), jnp.float32)

    def one_pair(pair_index):
        first_row = pair_index // arrived_count
        second_row = pair_index % arrived_count
        return lax.cond(
            link_rows[first_row, second_row] != 0,
            lambda: pair_cost(
                own_blocks[first_row],
                own_active[first_row],
                other_blocks[second_row],
                other_active[second_row],
                full_mask,
            ),
            lambda: jnp.zeros((columns,), jnp.float32),
        )

    pair_terms = lax.map(one_pair, jnp.arange(robots_here * arrived_count, dtype=jnp.int32))
    return pair_terms.reshape(robots_here, arrived_count, columns)


def seed_weights(centres, robot_cost):
    robots_here, _, spheres, columns = centres.shape
    seed_count = columns // W
    seed_cost = jnp.sum(robot_cost.reshape(robots_here, seed_count, W), axis=2)
    weight = 1.0 / (1.0 + seed_cost)
    shaped = centres.reshape(robots_here, 3, spheres, seed_count, W)
    weighted = jnp.sum(shaped * weight[:, None, None, :, None], axis=3)
    return (weighted, jnp.sum(weight, axis=1))


def local(centres, sphere_radius, counts, adjacency):
    own_blocks = swept_blocks(centres, sphere_radius)
    spheres = own_blocks.shape[2]
    robots_here = own_blocks.shape[0]
    own_active = active_spheres(counts, spheres)
    robot_cost = self_costs(own_blocks, own_active)
    group_size = lax.axis_size("robot")
    halfway = group_size // 2
    position = lax.axis_index("robot")
    order = jnp.arange(robots_here, dtype=jnp.int32)
    local_links = lax.dynamic_slice_in_dim(adjacency, position * robots_here, robots_here, 1)
    local_links = jnp.where(order[:, None] < order[None, :], local_links, 0)
    local_terms = cross_costs(own_blocks, own_active, own_blocks, own_active, local_links)
    robot_cost = robot_cost + jnp.sum(local_terms, axis=1) + jnp.sum(local_terms, axis=0)

    def turn(turn_index, state_now):
        totals_now, visiting, visiting_counts, returned = state_now
        visiting, visiting_counts, returned = shifted(
            (visiting, visiting_counts, returned), "robot", 1
        )
        anchor = (position - turn_index) % group_size
        taken = (turn_index < halfway) | (position < halfway)
        link_rows = lax.dynamic_slice_in_dim(adjacency, anchor * robots_here, robots_here, 1)
        link_rows = jnp.where(taken, link_rows, 0)
        pair_terms = cross_costs(
            own_blocks, own_active, visiting, active_spheres(visiting_counts, spheres), link_rows
        )
        return (
            totals_now + jnp.sum(pair_terms, axis=1),
            visiting,
            visiting_counts,
            returned + jnp.sum(pair_terms, axis=0),
        )

    start_state = (robot_cost, own_blocks, counts, jnp.zeros_like(robot_cost))
    robot_cost, _, _, returned = lax.fori_loop(1, halfway + 1, turn, start_state)
    robot_cost = robot_cost + shifted(returned, "robot", -halfway)
    weighted, totals = seed_weights(centres, robot_cost)
    weighted, totals = in_one((weighted, totals), "seed")
    return (robot_cost, weighted / totals[:, None, None, None])


def solution(mesh):
    return jax.shard_map(
        local,
        mesh=mesh,
        in_specs=(P("robot", None, None, "seed"), P("robot", None), P("robot"), P("robot", None)),
        out_specs=(P("robot", "seed"), P("robot", None, None, None)),
        check_vma=False,
    )
```

profile of v0, /device:TPU:2, one launch (start us, length us, event | category | flops | bytes accessed | tf_op | source)
XLA Modules:
  0.0 358.9 jit_solution(8242510251659695739)
XLA Ops:
  5.3 18.4 %while.118 = (s32[]{:T(128)}, f32[4,256]{1,0:T(4,128)S(1)}, s32[4]{0:T(128)S(1)}, s32[2,2]{1,0:T(2,128)S(1)}, f32[2,4,52,256]{3,2,1,0:T(8,128)S(1)}, /*index=5*/...) while((s32[]{:T(128)}, f32[4,256]{1,0:T(4,128)S(1)}, ...), condition=%wide.region_12.13_spmd.clone, body=%wide.region_6.12_spmd.clone.sunk | while | flops 4848652 | bytes 1520785 | solution.py:110
  23.7 16.2 %while.117 = (s32[]{:T(128)}, f32[2,256]{1,0:T(2,128)S(1)}, s32[2]{0:T(128)S(1)}, f32[2,4,52,256]{3,2,1,0:T(8,128)S(1)}, f32[2,52]{1,0:T(2,128)S(1)}, /*index=5*...) while((s32[]{:T(128)}, f32[2,256]{1,0:T(2,128)S(1)}, ...), condition=%wide.region_5.6_spmd.clone, body=%wide.region_1.5_spmd.clone.sunk | while | flops 4853822 | bytes 774118 | solution.py:85
  39.9 284.8 %while.120 = (s32[]{:T(128)}, f32[2,256]{1,0:T(2,128)S(1)}, f32[2,4,52,256]{3,2,1,0:T(8,128)S(1)}, s32[2]{0:T(128)S(1)}, f32[2,256]{1,0:T(2,128)S(1)}, /*index=5...) while((s32[]{:T(128)}, f32[2,256]{1,0:T(2,128)S(1)}, ...), condition=%wide.region_25.26_spmd.clone, body=%wide.region_15.25_spmd.clone.sunk | while | flops 4851445 | bytes 4118824 | solution.py:159
  48.3 24.0 %while.122 = (s32[]{:T(128)}, f32[4,256]{1,0:T(4,128)S(1)}, s32[4]{0:T(128)S(1)}, s32[2,2]{1,0:T(2,128)S(1)}, f32[2,4,52,256]{3,2,1,0:T(8,128)S(1)}, /*index=5*/...) while((s32[]{:T(128)}, f32[4,256]{1,0:T(4,128)S(1)}, ...), condition=%wide.region_22.22_spmd.clone, body=%wide.region_16.21_spmd.clone.sunk | while | flops 4848652 | bytes 1520817 | solution.py:110
  66.7 5.5 %conditional.7 = (f32[1,256]{1,0:T(1,128)S(1)}) conditional(s32[]{:T(128)} %bitcast.111, () %tuple.253, (s32[]{:T(128)}, f32[2,4,52,256]{3,2,1,0:T(8,128)S(1)}, s32[]{:T(128)}, f32[2,4,52,256]{3,2,1,0:T(8,128)S(1)}, f32[2,52]{1,0:T(2,128)S(1)}, /*index=5*/f32[2,52]{1,0:T(2,128)S(1)}) %tuple.254), branch_computations={%region_17.16_spmd, %region_18.20_spmd} | conditional | flops 4848415 | bytes 1517875 | solution.py:98
  80.5 24.0 %while.122 = (s32[]{:T(128)}, f32[4,256]{1,0:T(4,128)S(1)}, s32[4]{0:T(128)S(1)}, s32[2,2]{1,0:T(2,128)S(1)}, f32[2,4,52,256]{3,2,1,0:T(8,128)S(1)}, /*index=5*/...) while((s32[]{:T(128)}, f32[4,256]{1,0:T(4,128)S(1)}, ...), condition=%wide.region_22.22_spmd.clone, body=%wide.region_16.21_spmd.clone.sunk | while | flops 4848652 | bytes 1520817 | solution.py:110
  85.0 5.5 %conditional.7 = (f32[1,256]{1,0:T(1,128)S(1)}) conditional(s32[]{:T(128)} %bitcast.111, () %tuple.253, (s32[]{:T(128)}, f32[2,4,52,256]{3,2,1,0:T(8,128)S(1)}, s32[]{:T(128)}, f32[2,4,52,256]{3,2,1,0:T(8,128)S(1)}, f32[2,52]{1,0:T(2,128)S(1)}, /*index=5*/f32[2,52]{1,0:T(2,128)S(1)}) %tuple.254), branch_computations={%region_17.16_spmd, %region_18.20_spmd} | conditional | flops 4848415 | bytes 1517875 | solution.py:98
  105.3 6.2 %collective-permute-start.1 = (s32[2]{0:T(128)S(1)}, s32[2]{0:T(128)S(1)}, u32[]{:S(2)}, u32[]{:S(2)}) collective-permute-start(s32[2]{0:T(128)S(1)} %get-tuple-element.1705), channel_id=1, source_target_pairs={{240,0},{0,16},{16,32},{32,48},{48,64},{64,80},{80,96},{96,112},{1... | collective-permute-start | bytes 32 | tf_op jit(solution)/shard_map/while/body/eval_jaxpr/ppermute | solution.py:15
  111.5 10.2 %collective-permute-start.2 = (f32[2,256]{1,0:T(2,128)S(1)}, f32[2,256]{1,0:T(2,128)S(1)}, u32[]{:S(2)}, u32[]{:S(2)}) collective-permute-start(f32[2,256]{1,0:T(2,128)S(1)} %broadcast_select_fusion.2), channel_id=1, source_target_pairs={{240,0},{0,16},{16,32},{32,48},{48,64},{64,80},{80,96},{96,112},{1... | collective-permute-start | bytes 6152 | tf_op jit(solution)/shard_map/while/body/eval_jaxpr/ppermute | solution.py:15
  121.8 18.5 %while.122 = (s32[]{:T(128)}, f32[4,256]{1,0:T(4,128)S(1)}, s32[4]{0:T(128)S(1)}, s32[2,2]{1,0:T(2,128)S(1)}, f32[2,4,52,256]{3,2,1,0:T(8,128)S(1)}, /*index=5*/...) while((s32[]{:T(128)}, f32[4,256]{1,0:T(4,128)S(1)}, ...), condition=%wide.region_22.22_spmd.clone, body=%wide.region_16.21_spmd.clone.sunk | while | flops 4848652 | bytes 1520817 | solution.py:110
  140.4 6.1 %collective-permute-start = (f32[2,4,52,256]{3,2,1,0:T(8,128)S(1)}, f32[2,4,52,256]{3,2,1,0:T(8,128)S(1)}, u32[]{:S(2)}, u32[]{:S(2)}) collective-permute-start(f32[2,4,52,256]{3,2,1,0:T(8,128)S(1)} %get-tuple-element.1704), channel_id=1, source_target_pairs={{240,0},{0,16},{16,32},{32,48},{48,64},{64,80},{80,96},{96,112},{1... | collective-permute-start | bytes 1277960 | tf_op jit(solution)/shard_map/while/body/eval_jaxpr/ppermute | solution.py:15
  146.5 14.2 %collective-permute-start.1 = (s32[2]{0:T(128)S(1)}, s32[2]{0:T(128)S(1)}, u32[]{:S(2)}, u32[]{:S(2)}) collective-permute-start(s32[2]{0:T(128)S(1)} %get-tuple-element.1705), channel_id=1, source_target_pairs={{240,0},{0,16},{16,32},{32,48},{48,64},{64,80},{80,96},{96,112},{1... | collective-permute-start | bytes 32 | tf_op jit(solution)/shard_map/while/body/eval_jaxpr/ppermute | solution.py:15
  161.5 18.5 %while.122 = (s32[]{:T(128)}, f32[4,256]{1,0:T(4,128)S(1)}, s32[4]{0:T(128)S(1)}, s32[2,2]{1,0:T(2,128)S(1)}, f32[2,4,52,256]{3,2,1,0:T(8,128)S(1)}, /*index=5*/...) while((s32[]{:T(128)}, f32[4,256]{1,0:T(4,128)S(1)}, ...), condition=%wide.region_22.22_spmd.clone, body=%wide.region_16.21_spmd.clone.sunk | while | flops 4848652 | bytes 1520817 | solution.py:110
  180.1 10.2 %collective-permute-start = (f32[2,4,52,256]{3,2,1,0:T(8,128)S(1)}, f32[2,4,52,256]{3,2,1,0:T(8,128)S(1)}, u32[]{:S(2)}, u32[]{:S(2)}) collective-permute-start(f32[2,4,52,256]{3,2,1,0:T(8,128)S(1)} %get-tuple-element.1704), channel_id=1, source_target_pairs={{240,0},{0,16},{16,32},{32,48},{48,64},{64,80},{80,96},{96,112},{1... | collective-permute-start | bytes 1277960 | tf_op jit(solution)/shard_map/while/body/eval_jaxpr/ppermute | solution.py:15
  193.4 24.0 %while.122 = (s32[]{:T(128)}, f32[4,256]{1,0:T(4,128)S(1)}, s32[4]{0:T(128)S(1)}, s32[2,2]{1,0:T(2,128)S(1)}, f32[2,4,52,256]{3,2,1,0:T(8,128)S(1)}, /*index=5*/...) while((s32[]{:T(128)}, f32[4,256]{1,0:T(4,128)S(1)}, ...), condition=%wide.region_22.22_spmd.clone, body=%wide.region_16.21_spmd.clone.sunk | while | flops 4848652 | bytes 1520817 | solution.py:110
  197.9 5.5 %conditional.7 = (f32[1,256]{1,0:T(1,128)S(1)}) conditional(s32[]{:T(128)} %bitcast.111, () %tuple.253, (s32[]{:T(128)}, f32[2,4,52,256]{3,2,1,0:T(8,128)S(1)}, s32[]{:T(128)}, f32[2,4,52,256]{3,2,1,0:T(8,128)S(1)}, f32[2,52]{1,0:T(2,128)S(1)}, /*index=5*/f32[2,52]{1,0:T(2,128)S(1)}) %tuple.254), branch_computations={%region_17.16_spmd, %region_18.20_spmd} | conditional | flops 4848415 | bytes 1517875 | solution.py:98
  217.6 11.4 %collective-permute-start.1 = (s32[2]{0:T(128)S(1)}, s32[2]{0:T(128)S(1)}, u32[]{:S(2)}, u32[]{:S(2)}) collective-permute-start(s32[2]{0:T(128)S(1)} %get-tuple-element.1705), channel_id=1, source_target_pairs={{240,0},{0,16},{16,32},{32,48},{48,64},{64,80},{80,96},{96,112},{1... | collective-permute-start | bytes 32 | tf_op jit(solution)/shard_map/while/body/eval_jaxpr/ppermute | solution.py:15
  229.8 18.5 %while.122 = (s32[]{:T(128)}, f32[4,256]{1,0:T(4,128)S(1)}, s32[4]{0:T(128)S(1)}, s32[2,2]{1,0:T(2,128)S(1)}, f32[2,4,52,256]{3,2,1,0:T(8,128)S(1)}, /*index=5*/...) while((s32[]{:T(128)}, f32[4,256]{1,0:T(4,128)S(1)}, ...), condition=%wide.region_22.22_spmd.clone, body=%wide.region_16.21_spmd.clone.sunk | while | flops 4848652 | bytes 1520817 | solution.py:110
  253.1 14.5 %collective-permute-start.1 = (s32[2]{0:T(128)S(1)}, s32[2]{0:T(128)S(1)}, u32[]{:S(2)}, u32[]{:S(2)}) collective-permute-start(s32[2]{0:T(128)S(1)} %get-tuple-element.1705), channel_id=1, source_target_pairs={{240,0},{0,16},{16,32},{32,48},{48,64},{64,80},{80,96},{96,112},{1... | collective-permute-start | bytes 32 | tf_op jit(solution)/shard_map/while/body/eval_jaxpr/ppermute | solution.py:15
  268.4 24.0 %while.122 = (s32[]{:T(128)}, f32[4,256]{1,0:T(4,128)S(1)}, s32[4]{0:T(128)S(1)}, s32[2,2]{1,0:T(2,128)S(1)}, f32[2,4,52,256]{3,2,1,0:T(8,128)S(1)}, /*index=5*/...) while((s32[]{:T(128)}, f32[4,256]{1,0:T(4,128)S(1)}, ...), condition=%wide.region_22.22_spmd.clone, body=%wide.region_16.21_spmd.clone.sunk | while | flops 4848652 | bytes 1520817 | solution.py:110
  273.0 5.5 %conditional.7 = (f32[1,256]{1,0:T(1,128)S(1)}) conditional(s32[]{:T(128)} %bitcast.111, () %tuple.253, (s32[]{:T(128)}, f32[2,4,52,256]{3,2,1,0:T(8,128)S(1)}, s32[]{:T(128)}, f32[2,4,52,256]{3,2,1,0:T(8,128)S(1)}, f32[2,52]{1,0:T(2,128)S(1)}, /*index=5*/f32[2,52]{1,0:T(2,128)S(1)}) %tuple.254), branch_computations={%region_17.16_spmd, %region_18.20_spmd} | conditional | flops 4848415 | bytes 1517875 | solution.py:98
  300.6 24.0 %while.122 = (s32[]{:T(128)}, f32[4,256]{1,0:T(4,128)S(1)}, s32[4]{0:T(128)S(1)}, s32[2,2]{1,0:T(2,128)S(1)}, f32[2,4,52,256]{3,2,1,0:T(8,128)S(1)}, /*index=5*/...) while((s32[]{:T(128)}, f32[4,256]{1,0:T(4,128)S(1)}, ...), condition=%wide.region_22.22_spmd.clone, body=%wide.region_16.21_spmd.clone.sunk | while | flops 4848652 | bytes 1520817 | solution.py:110
  309.8 5.5 %conditional.7 = (f32[1,256]{1,0:T(1,128)S(1)}) conditional(s32[]{:T(128)} %bitcast.111, () %tuple.253, (s32[]{:T(128)}, f32[2,4,52,256]{3,2,1,0:T(8,128)S(1)}, s32[]{:T(128)}, f32[2,4,52,256]{3,2,1,0:T(8,128)S(1)}, f32[2,52]{1,0:T(2,128)S(1)}, /*index=5*/f32[2,52]{1,0:T(2,128)S(1)}) %tuple.254), branch_computations={%region_17.16_spmd, %region_18.20_spmd} | conditional | flops 4848415 | bytes 1517875 | solution.py:98
  331.0 26.5 %all_to_all.6 = f32[16,1,9986]{2,1,0:T(1,128)S(1)} all-to-all(f32[16,1,9986]{2,1,0:T(1,128)S(1)} %broadcast_in_dim.66), channel_id=1, replica_groups=mesh['robot'=16,'seed'=16] {'seed'}, dimensions={0} | all-to-all | bytes 1278208 | tf_op jit(solution)/shard_map/all_to_all | solution.py:20
  (499 shorter events, 167.0 us)
Async XLA Ops:
  39.9 8.4 %collective-permute-start = (f32[2,4,52,256]{3,2,1,0:T(8,128)S(1)}, f32[2,4,52,256]{3,2,1,0:T(8,128)S(1)}, u32[]{:S(2)}, u32[]{:S(2)}) collective-permute-start(f32[2,4,52,256]{3,2,1,0:T(8,128)S(1)} %get-tuple-element.1704), channel_id=1, source_target_pairs={{240,0},{0,16},{16,32},{32,48},{48,64},{64,80},{80,96},{96,112},{1... | collective-permute-start | bytes 1277960 | tf_op jit(solution)/shard_map/while/body/eval_jaxpr/ppermute | solution.py:15
  45.3 3.0 collective-permute-start.1
  47.1 25.3 %collective-permute-start.2 = (f32[2,256]{1,0:T(2,128)S(1)}, f32[2,256]{1,0:T(2,128)S(1)}, u32[]{:S(2)}, u32[]{:S(2)}) collective-permute-start(f32[2,256]{1,0:T(2,128)S(1)} %broadcast_select_fusion.2), channel_id=1, source_target_pairs={{240,0},{0,16},{16,32},{32,48},{48,64},{64,80},{80,96},{96,112},{1... | collective-permute-start | bytes 6152 | tf_op jit(solution)/shard_map/while/body/eval_jaxpr/ppermute | solution.py:15
  72.4 8.1 %collective-permute-start = (f32[2,4,52,256]{3,2,1,0:T(8,128)S(1)}, f32[2,4,52,256]{3,2,1,0:T(8,128)S(1)}, u32[]{:S(2)}, u32[]{:S(2)}) collective-permute-start(f32[2,4,52,256]{3,2,1,0:T(8,128)S(1)} %get-tuple-element.1704), channel_id=1, source_target_pairs={{240,0},{0,16},{16,32},{32,48},{48,64},{64,80},{80,96},{96,112},{1... | collective-permute-start | bytes 1277960 | tf_op jit(solution)/shard_map/while/body/eval_jaxpr/ppermute | solution.py:15
  72.5 8.0 %collective-permute-start.1 = (s32[2]{0:T(128)S(1)}, s32[2]{0:T(128)S(1)}, u32[]{:S(2)}, u32[]{:S(2)}) collective-permute-start(s32[2]{0:T(128)S(1)} %get-tuple-element.1705), channel_id=1, source_target_pairs={{240,0},{0,16},{16,32},{32,48},{48,64},{64,80},{80,96},{96,112},{1... | collective-permute-start | bytes 32 | tf_op jit(solution)/shard_map/while/body/eval_jaxpr/ppermute | solution.py:15
  74.7 29.9 %collective-permute-start.2 = (f32[2,256]{1,0:T(2,128)S(1)}, f32[2,256]{1,0:T(2,128)S(1)}, u32[]{:S(2)}, u32[]{:S(2)}) collective-permute-start(f32[2,256]{1,0:T(2,128)S(1)} %broadcast_select_fusion.2), channel_id=1, source_target_pairs={{240,0},{0,16},{16,32},{32,48},{48,64},{64,80},{80,96},{96,112},{1... | collective-permute-start | bytes 6152 | tf_op jit(solution)/shard_map/while/body/eval_jaxpr/ppermute | solution.py:15
  104.6 17.2 %collective-permute-start = (f32[2,4,52,256]{3,2,1,0:T(8,128)S(1)}, f32[2,4,52,256]{3,2,1,0:T(8,128)S(1)}, u32[]{:S(2)}, u32[]{:S(2)}) collective-permute-start(f32[2,4,52,256]{3,2,1,0:T(8,128)S(1)} %get-tuple-element.1704), channel_id=1, source_target_pairs={{240,0},{0,16},{16,32},{32,48},{48,64},{64,80},{80,96},{96,112},{1... | collective-permute-start | bytes 1277960 | tf_op jit(solution)/shard_map/while/body/eval_jaxpr/ppermute | solution.py:15
  105.3 16.5 %collective-permute-start.1 = (s32[2]{0:T(128)S(1)}, s32[2]{0:T(128)S(1)}, u32[]{:S(2)}, u32[]{:S(2)}) collective-permute-start(s32[2]{0:T(128)S(1)} %get-tuple-element.1705), channel_id=1, source_target_pairs={{240,0},{0,16},{16,32},{32,48},{48,64},{64,80},{80,96},{96,112},{1... | collective-permute-start | bytes 32 | tf_op jit(solution)/shard_map/while/body/eval_jaxpr/ppermute | solution.py:15
  111.5 28.9 %collective-permute-start.2 = (f32[2,256]{1,0:T(2,128)S(1)}, f32[2,256]{1,0:T(2,128)S(1)}, u32[]{:S(2)}, u32[]{:S(2)}) collective-permute-start(f32[2,256]{1,0:T(2,128)S(1)} %broadcast_select_fusion.2), channel_id=1, source_target_pairs={{240,0},{0,16},{16,32},{32,48},{48,64},{64,80},{80,96},{96,112},{1... | collective-permute-start | bytes 6152 | tf_op jit(solution)/shard_map/while/body/eval_jaxpr/ppermute | solution.py:15
  140.4 21.2 %collective-permute-start = (f32[2,4,52,256]{3,2,1,0:T(8,128)S(1)}, f32[2,4,52,256]{3,2,1,0:T(8,128)S(1)}, u32[]{:S(2)}, u32[]{:S(2)}) collective-permute-start(f32[2,4,52,256]{3,2,1,0:T(8,128)S(1)} %get-tuple-element.1704), channel_id=1, source_target_pairs={{240,0},{0,16},{16,32},{32,48},{48,64},{64,80},{80,96},{96,112},{1... | collective-permute-start | bytes 1277960 | tf_op jit(solution)/shard_map/while/body/eval_jaxpr/ppermute | solution.py:15
  146.5 15.0 %collective-permute-start.1 = (s32[2]{0:T(128)S(1)}, s32[2]{0:T(128)S(1)}, u32[]{:S(2)}, u32[]{:S(2)}) collective-permute-start(s32[2]{0:T(128)S(1)} %get-tuple-element.1705), channel_id=1, source_target_pairs={{240,0},{0,16},{16,32},{32,48},{48,64},{64,80},{80,96},{96,112},{1... | collective-permute-start | bytes 32 | tf_op jit(solution)/shard_map/while/body/eval_jaxpr/ppermute | solution.py:15
  160.7 19.4 %collective-permute-start.2 = (f32[2,256]{1,0:T(2,128)S(1)}, f32[2,256]{1,0:T(2,128)S(1)}, u32[]{:S(2)}, u32[]{:S(2)}) collective-permute-start(f32[2,256]{1,0:T(2,128)S(1)} %broadcast_select_fusion.2), channel_id=1, source_target_pairs={{240,0},{0,16},{16,32},{32,48},{48,64},{64,80},{80,96},{96,112},{1... | collective-permute-start | bytes 6152 | tf_op jit(solution)/shard_map/while/body/eval_jaxpr/ppermute | solution.py:15
  180.1 13.2 %collective-permute-start = (f32[2,4,52,256]{3,2,1,0:T(8,128)S(1)}, f32[2,4,52,256]{3,2,1,0:T(8,128)S(1)}, u32[]{:S(2)}, u32[]{:S(2)}) collective-permute-start(f32[2,4,52,256]{3,2,1,0:T(8,128)S(1)} %get-tuple-element.1704), channel_id=1, source_target_pairs={{240,0},{0,16},{16,32},{32,48},{48,64},{64,80},{80,96},{96,112},{1... | collective-permute-start | bytes 1277960 | tf_op jit(solution)/shard_map/while/body/eval_jaxpr/ppermute | solution.py:15
  190.5 27.0 %collective-permute-start.2 = (f32[2,256]{1,0:T(2,128)S(1)}, f32[2,256]{1,0:T(2,128)S(1)}, u32[]{:S(2)}, u32[]{:S(2)}) collective-permute-start(f32[2,256]{1,0:T(2,128)S(1)} %broadcast_select_fusion.2), channel_id=1, source_target_pairs={{240,0},{0,16},{16,32},{32,48},{48,64},{64,80},{80,96},{96,112},{1... | collective-permute-start | bytes 6152 | tf_op jit(solution)/shard_map/while/body/eval_jaxpr/ppermute | solution.py:15
  217.5 12.3 %collective-permute-start = (f32[2,4,52,256]{3,2,1,0:T(8,128)S(1)}, f32[2,4,52,256]{3,2,1,0:T(8,128)S(1)}, u32[]{:S(2)}, u32[]{:S(2)}) collective-permute-start(f32[2,4,52,256]{3,2,1,0:T(8,128)S(1)} %get-tuple-element.1704), channel_id=1, source_target_pairs={{240,0},{0,16},{16,32},{32,48},{48,64},{64,80},{80,96},{96,112},{1... | collective-permute-start | bytes 1277960 | tf_op jit(solution)/shard_map/while/body/eval_jaxpr/ppermute | solution.py:15
  217.6 12.2 %collective-permute-start.1 = (s32[2]{0:T(128)S(1)}, s32[2]{0:T(128)S(1)}, u32[]{:S(2)}, u32[]{:S(2)}) collective-permute-start(s32[2]{0:T(128)S(1)} %get-tuple-element.1705), channel_id=1, source_target_pairs={{240,0},{0,16},{16,32},{32,48},{48,64},{64,80},{80,96},{96,112},{1... | collective-permute-start | bytes 32 | tf_op jit(solution)/shard_map/while/body/eval_jaxpr/ppermute | solution.py:15
  229.0 19.4 %collective-permute-start.2 = (f32[2,256]{1,0:T(2,128)S(1)}, f32[2,256]{1,0:T(2,128)S(1)}, u32[]{:S(2)}, u32[]{:S(2)}) collective-permute-start(f32[2,256]{1,0:T(2,128)S(1)} %broadcast_select_fusion.2), channel_id=1, source_target_pairs={{240,0},{0,16},{16,32},{32,48},{48,64},{64,80},{80,96},{96,112},{1... | collective-permute-start | bytes 6152 | tf_op jit(solution)/shard_map/while/body/eval_jaxpr/ppermute | solution.py:15
  248.4 20.0 %collective-permute-start = (f32[2,4,52,256]{3,2,1,0:T(8,128)S(1)}, f32[2,4,52,256]{3,2,1,0:T(8,128)S(1)}, u32[]{:S(2)}, u32[]{:S(2)}) collective-permute-start(f32[2,4,52,256]{3,2,1,0:T(8,128)S(1)} %get-tuple-element.1704), channel_id=1, source_target_pairs={{240,0},{0,16},{16,32},{32,48},{48,64},{64,80},{80,96},{96,112},{1... | collective-permute-start | bytes 1277960 | tf_op jit(solution)/shard_map/while/body/eval_jaxpr/ppermute | solution.py:15
  253.1 15.3 %collective-permute-start.1 = (s32[2]{0:T(128)S(1)}, s32[2]{0:T(128)S(1)}, u32[]{:S(2)}, u32[]{:S(2)}) collective-permute-start(s32[2]{0:T(128)S(1)} %get-tuple-element.1705), channel_id=1, source_target_pairs={{240,0},{0,16},{16,32},{32,48},{48,64},{64,80},{80,96},{96,112},{1... | collective-permute-start | bytes 32 | tf_op jit(solution)/shard_map/while/body/eval_jaxpr/ppermute | solution.py:15
  267.6 24.9 %collective-permute-start.2 = (f32[2,256]{1,0:T(2,128)S(1)}, f32[2,256]{1,0:T(2,128)S(1)}, u32[]{:S(2)}, u32[]{:S(2)}) collective-permute-start(f32[2,256]{1,0:T(2,128)S(1)} %broadcast_select_fusion.2), channel_id=1, source_target_pairs={{240,0},{0,16},{16,32},{32,48},{48,64},{64,80},{80,96},{96,112},{1... | collective-permute-start | bytes 6152 | tf_op jit(solution)/shard_map/while/body/eval_jaxpr/ppermute | solution.py:15
  292.5 8.1 %collective-permute-start = (f32[2,4,52,256]{3,2,1,0:T(8,128)S(1)}, f32[2,4,52,256]{3,2,1,0:T(8,128)S(1)}, u32[]{:S(2)}, u32[]{:S(2)}) collective-permute-start(f32[2,4,52,256]{3,2,1,0:T(8,128)S(1)} %get-tuple-element.1704), channel_id=1, source_target_pairs={{240,0},{0,16},{16,32},{32,48},{48,64},{64,80},{80,96},{96,112},{1... | collective-permute-start | bytes 1277960 | tf_op jit(solution)/shard_map/while/body/eval_jaxpr/ppermute | solution.py:15
  297.3 3.4 collective-permute-start.1
  297.4 27.3 %collective-permute-start.2 = (f32[2,256]{1,0:T(2,128)S(1)}, f32[2,256]{1,0:T(2,128)S(1)}, u32[]{:S(2)}, u32[]{:S(2)}) collective-permute-start(f32[2,256]{1,0:T(2,128)S(1)} %broadcast_select_fusion.2), channel_id=1, source_target_pairs={{240,0},{0,16},{16,32},{32,48},{48,64},{64,80},{80,96},{96,112},{1... | collective-permute-start | bytes 6152 | tf_op jit(solution)/shard_map/while/body/eval_jaxpr/ppermute | solution.py:15
  324.7 5.2 %collective-permute-start.3 = (f32[2,256]{1,0:T(2,128)S(1)}, f32[2,256]{1,0:T(2,128)S(1)}, u32[]{:S(2)}, u32[]{:S(2)}) collective-permute-start(f32[2,256]{1,0:T(2,128)S(1)} %get-tuple-element.653), channel_id=1, source_target_pairs={{128,0},{144,16},{160,32},{176,48},{192,64},{208,80},{224,96},{240... | collective-permute-start | bytes 6152 | tf_op jit(solution)/shard_map/ppermute | solution.py:15
  (5 other events, 6.1 us)
where the time goes:
time: 366 us; the launch traced here: 359 us
  loops' own time  130 us (36%)
  starting transfers between devices  97 us (27%)
  local copies, waits for them, and re-layouts  63.7 us (17%)
  blocking collectives  26.5 us (7%)
  other arithmetic  25.2 us (7%)
  waiting for transfers between devices  15.4 us (4%)
    another operation x9, loops' own time, cross_costs(): lax.map(one_pair, jnp.arange(robots_here * arrived_count, dtype=jnp.int32))  116 us
    ppermute x25, starting transfers between devices, shifted(): return lax.ppermute(block, axis, route)  97 us
    all_to_all x1, blocking collectives, sent_to_all(): return lax.all_to_all(copies, axis, split_axis=0, concat_axis=0, tiled=True)  26.5 us
    dynamic_slice x36, local copies, waits for them, and re-layouts, one_pair(): link_rows[first_row, second_row] != 0  23.1 us
    dynamic_slice x36, local copies, waits for them, and re-layouts, cross_costs(): lax.map(one_pair, jnp.arange(robots_here * arrived_count, dtype=jnp.int32))  22.2 us
    reduce_sum x14, other arithmetic, tile_cost(): jnp.sum(weights[:, :, None] * jnp.exp(-distance / (spread * spread)), axi...  18.4 us
    ppermute x25, waiting for transfers between devices, shifted(): return lax.ppermute(block, axis, route)  15.4 us
    dynamic_slice x16, local copies, waits for them, and re-layouts, self_costs(): return lax.map(single, jnp.arange(own_blocks.shape[0], dtype=jnp.int32))  9.79 us
  transfers between devices with their start and end apart: 25, of which 8 were waited for; matrix products, arithmetic and copies ran while one was open for 19% of the time, Pallas kernels for 0%

commit v1 on v0

v1 whole, which is shorter than its diff:
```python
import functools
import math

import jax
import jax.numpy as jnp
from jax import lax
from jax.experimental import pallas as pl
from jax.experimental.pallas import tpu as pltpu
from jax.sharding import PartitionSpec as P

W = 32
SPHERES = 52
GROUPS = 7
FIRST_GROUPS = 4
ROBOTS_HERE = 2
ROBOT_DEVICES = 16
ROBOTS = ROBOTS_HERE * ROBOT_DEVICES
LANES = 128
COLUMNS = 256
PART = 16
ROWS = ROBOTS_HERE * GROUPS * 4
Z = 8
CHUNK = 11
COUNT_LANE = 32
LENGTH_LANE = 32
GROUPS_LANE = 33
ROOT = math.sqrt(math.log2(math.e))
FAR = 1.0e6
MESH = pl.DeviceIdType.MESH


def iota(axis, shape=(8, LANES)):
    return lax.broadcasted_iota(jnp.int32, shape, axis)


def pair_term(a, b):
    dx, dy, dz = a[0] - b[0], a[1] - b[1], a[2] - b[2]
    spread = a[3] + b[3]
    return jnp.exp2((dx * dx + dy * dy + dz * dz) / (-spread * spread))


def spread_kernel(
    counts_ref,
    centres_ref,
    radius_ref,
    adjacency_ref,
    recv_ref,
    self_ref,
    table_ref,
    send,
    swept,
    note_send,
    note_recv,
    note,
    send_sem,
    recv_sem,
    note_send_sem,
    note_recv_sem,
):
    me = lax.axis_index("robot")
    seed = lax.axis_index("seed")
    peers = [lax.rem(me + step, ROBOT_DEVICES) for step in range(1, ROBOT_DEVICES)]

    barrier = pltpu.get_barrier_semaphore()
    for peer in peers:
        pl.semaphore_signal(barrier, inc=1, device_id=(peer, seed), device_id_type=MESH)

    sub, lane = iota(0), iota(1)
    part = lane // PART
    last_waypoint = lane % W == W - 1
    radius_lane = iota(1, (8, SPHERES))
    radius_sub = iota(0, (8, SPHERES))
    for robot in range(ROBOTS_HERE):
        count = counts_ref[robot]
        radius_row = jnp.broadcast_to(radius_ref[robot : robot + 1, :], (8, SPHERES))
        number = (me * ROBOTS_HERE + robot) * 64 + 1
        for group in range(GROUPS):
            radius = jnp.sum(
                jnp.where(radius_lane == radius_sub + 8 * group, radius_row, 0.0),
                axis=1,
                keepdims=True,
            )
            sphere = sub + 8 * group
            active = sphere < count
            far = FAR * (sphere + number).astype(jnp.float32)
            for half in range(2):
                at = slice(half * LANES, (half + 1) * LANES)
                out, square = [], None
                for axis in range(3):
                    if group < GROUPS - 1:
                        here = centres_ref[robot, axis, 8 * group : 8 * group + 8, at]
                    else:
                        here = pltpu.roll(
                            centres_ref[robot, axis, SPHERES - 8 : SPHERES, at], 4, 0
                        )
                    ahead = jnp.where(last_waypoint, here, pltpu.roll(here, LANES - 1, 1))
                    step = ahead - here
                    square = step * step if square is None else square + step * step
                    middle = (here + ahead) * (0.5 * ROOT)
                    out.append(jnp.where(active, middle, far if axis == 0 else 0.0))
                out.append(jnp.where(active, radius + 0.5 * jnp.sqrt(square + 1e-6), 1.0))
                for quantity in range(4):
                    value = out[quantity]
                    swept[half * ROBOTS_HERE + robot, quantity, 8 * group : 8 * group + 8, :] = value
                    value = pltpu.roll(value, 0, 1, stride=PART, stride_axis=0)
                    for bit in (1, 2, 4):
                        value = jnp.where(part & bit != 0, pltpu.roll(value, 8 - bit, 0), value)
                    row = (robot * GROUPS + group) * 4 + quantity
                    send[pl.ds(half * 8 * ROWS + row, 8, stride=ROWS), :] = value
        for half in range(2):
            for quantity in range(4):
                fill = FAR * (sub + 56 + number).astype(jnp.float32) if quantity == 0 else jnp.full((8, LANES), float(quantity == 3))
                swept[half * ROBOTS_HERE + robot, quantity, 56:64, :] = fill

    note_send[...] = jnp.zeros((ROBOTS_HERE, LANES), jnp.int32)
    note_send[:, 0:ROBOTS] = adjacency_ref[...]
    for robot in range(ROBOTS_HERE):
        note_send[robot : robot + 1, COUNT_LANE : COUNT_LANE + 1] = jnp.full((1, 1), counts_ref[robot], jnp.int32)

    pl.semaphore_wait(barrier, ROBOT_DEVICES - 1)

    def slot_of(device):
        return (device // 8) * 8 + lax.rem(8 - lax.rem(device, 8), 8)

    def rows_of(slot):
        return pl.ds(pl.multiple_of(slot * ROWS, 8), ROWS)

    notes, copies = [], []
    for number, peer in enumerate(peers):
        copy = pltpu.make_async_remote_copy(
            src_ref=note_send,
            dst_ref=note_recv.at[me],
            send_sem=note_send_sem.at[number],
            recv_sem=note_recv_sem.at[number],
            device_id=(peer, seed),
            device_id_type=MESH,
        )
        copy.start()
        notes.append(copy)
    for number, peer in enumerate(peers):
        copy = pltpu.make_async_remote_copy(
            src_ref=send.at[rows_of(slot_of(peer))],
            dst_ref=recv_ref.at[rows_of(me)],
            send_sem=send_sem.at[number],
            recv_sem=recv_sem.at[number],
            device_id=(peer, seed),
            device_id_type=MESH,
        )
        copy.start()
        copies.append(copy)
    note_recv[me] = note_send[...]
    recv_ref[rows_of(me), :] = send[rows_of(slot_of(me)), :]

    def self_pairs(index, carry):
        half, robot = index // ROBOTS_HERE, lax.rem(index, ROBOTS_HERE)
        sums = [jnp.zeros((8, LANES), jnp.float32) for _ in range(4)]
        turn = 0
        for group in range(GROUPS):
            first = [swept[index, q, 8 * group : 8 * group + 8, :] for q in range(4)]
            for apart in range(2, SPHERES - 8 * group):
                start = 8 * group + apart
                second = [swept[index, q, start : start + 8, :] for q in range(4)]
                sums[turn] = sums[turn] + pair_term(first, second)
                turn = (turn + 1) % 4
        total = jnp.sum((sums[0] + sums[1]) + (sums[2] + sums[3]), axis=0, keepdims=True)
        self_ref[pl.ds(index, 1), :] = total * (1.0 / (SPHERES * SPHERES))
        return carry

    lax.fori_loop(0, 2 * ROBOTS_HERE, self_pairs, 0)

    for copy in notes:
        copy.wait_recv()
    for device in range(ROBOT_DEVICES):
        note[ROBOTS_HERE * device : ROBOTS_HERE * (device + 1), :] = note_recv[device]
    shape = (ROBOTS, LANES)
    row, column = iota(0, shape), iota(1, shape)
    noted = note[...].astype(jnp.float32)
    link = jnp.where((column > row) & (column < ROBOTS) & (noted != 0.0), 1.0, 0.0)
    counts = jnp.sum(jnp.where(column == COUNT_LANE, noted, 0.0), axis=1, keepdims=True)
    before = (iota(0, (LANES, LANES)) < iota(1, (LANES, LANES))).astype(jnp.float32)
    rank = jnp.dot(link, before, preferred_element_type=jnp.float32)
    linked_column = link * column.astype(jnp.float32)
    table = jnp.zeros(shape, jnp.float32)
    for place in range(ROBOTS - 1):
        found = jnp.sum(jnp.where(rank == float(place), linked_column, 0.0), axis=1, keepdims=True)
        table = jnp.where(column == place, found, table)
    table = jnp.where(column == LENGTH_LANE, jnp.sum(link, axis=1, keepdims=True), table)
    table = table.astype(jnp.int32)
    groups = (counts.astype(jnp.int32) + 7) >> 3
    table_ref[...] = jnp.where(column == GROUPS_LANE, groups, table)

    for copy in copies:
        copy.wait_recv()
    for copy in notes + copies:
        copy.wait_send()


def cross_kernel(table, rows, cost_ref, turned, total):
    def prepare(robot, carry):
        for row in range(4 * GROUPS):
            line = rows[pl.ds(robot * (4 * GROUPS) + row, 1), :]
            turned[robot, row] = pltpu.roll(
                jnp.broadcast_to(line, (8, LANES)), 0, 1, stride=PART, stride_axis=0
            )
        total[robot] = jnp.zeros((8, LANES), jnp.float32)
        return carry

    lax.fori_loop(0, ROBOTS, prepare, 0)

    def pair_sum(first_groups, second_groups, first, second):
        sums = [None] * 4
        turn = 0
        for second_group in range(second_groups):
            b = [
                jnp.broadcast_to(
                    rows[pl.ds(second * (4 * GROUPS) + second_group * 4 + q, 1), :], (8, LANES)
                )
                for q in range(4)
            ]
            for first_group in range(first_groups):
                a = [turned[first, first_group * 4 + q] for q in range(4)]
                term = pair_term(a, b)
                sums[turn] = term if sums[turn] is None else sums[turn] + term
                turn = (turn + 1) % 4
        return (sums[0] + sums[1]) + (sums[2] + sums[3])

    def of_robot(first, carry):
        first_groups = table[first, GROUPS_LANE]

        def of_pair(place, carry):
            second = table[first, place]
            second_groups = table[second, GROUPS_LANE]
            case = (first_groups - FIRST_GROUPS) * 4 + (second_groups - FIRST_GROUPS)
            found = lax.switch(
                case,
                [
                    functools.partial(pair_sum, m, n)
                    for m in range(FIRST_GROUPS, GROUPS + 1)
                    for n in range(FIRST_GROUPS, GROUPS + 1)
                ],
                first,
                second,
            )
            total[first] = total[first] + found
            total[second] = total[second] + found
            return carry

        return lax.fori_loop(0, table[first, LENGTH_LANE], of_pair, carry)

    lax.fori_loop(0, ROBOTS, of_robot, 0)

    cost = jnp.sum(total[...], axis=1)
    for shift in (64, 32, 16):
        cost = cost + pltpu.roll(cost, shift, 1)
    cost = cost * (1.0 / (SPHERES * SPHERES))
    for device in range(ROBOT_DEVICES):
        cost_ref[device] = cost[ROBOTS_HERE * device : ROBOTS_HERE * (device + 1), :]


def blend_kernel(
    cost_ref,
    self_ref,
    centres_ref,
    robot_cost_ref,
    blended_ref,
    cost_recv,
    weight,
    packed,
    parts,
    mine,
    other,
    gathered,
    cost_sems,
    part_sems,
    pair_sems,
    gather_sems,
):
    me = lax.axis_index("robot")
    seed = lax.axis_index("seed")
    x, z = seed // Z, lax.rem(seed, Z)
    peers = [lax.rem(me + step, ROBOT_DEVICES) for step in range(1, ROBOT_DEVICES)]
    z_peers = [lax.rem(z + step, Z) for step in range(1, Z)]
    opposite = (1 - x) * Z + z

    barrier = pltpu.get_barrier_semaphore()
    for peer in peers:
        pl.semaphore_signal(barrier, inc=1, device_id=(peer, seed), device_id_type=MESH)
    for peer in z_peers:
        pl.semaphore_signal(barrier, inc=1, device_id=(me, x * Z + peer), device_id_type=MESH)
    pl.semaphore_signal(barrier, inc=1, device_id=(me, opposite), device_id_type=MESH)
    pl.semaphore_wait(barrier, ROBOT_DEVICES - 1 + Z)

    def start(src, dst, sems, number, device):
        copy = pltpu.make_async_remote_copy(
            src_ref=src,
            dst_ref=dst,
            send_sem=sems.at[0, number],
            recv_sem=sems.at[1, number],
            device_id=device,
            device_id_type=MESH,
        )
        copy.start()
        return copy

    copies = [
        start(cost_ref.at[peer], cost_recv.at[me], cost_sems, number, (peer, seed))
        for number, peer in enumerate(peers)
    ]
    cost_recv[me] = cost_ref[me]
    for copy in copies:
        copy.wait_recv()
    sent = copies

    lane = iota(1, (ROBOTS_HERE, LANES))
    part = lane // PART
    for half in range(2):
        cost = self_ref[half * ROBOTS_HERE : (half + 1) * ROBOTS_HERE, :]
        for k in range(8):
            cost = cost + jnp.where(part == k, cost_recv[half * 8 + k], 0.0)
        robot_cost_ref[:, half * LANES : (half + 1) * LANES] = cost
        for bit in (1, 2, 4, 8, 16):
            cost = cost + jnp.where(
                lane & bit != 0, pltpu.roll(cost, bit, 1), pltpu.roll(cost, LANES - bit, 1)
            )
        weight[half] = 1.0 / (1.0 + cost)
    sums = weight[0] + weight[1]
    sums = sums + pltpu.roll(sums, 64, 1)
    sums = sums + pltpu.roll(sums, 32, 1)
    line = iota(1, (1, LANES))
    total_row = jnp.where(line < 64, sums[0:1, :], sums[1:2, :])

    quarter = iota(1) // W
    units = [[], []]
    for robot in range(ROBOTS_HERE):
        weights = [
            jnp.broadcast_to(weight[half, robot : robot + 1, :], (8, LANES)) for half in range(2)
        ]
        for axis in range(3):
            for group in range(GROUPS):
                start_row = min(8 * group, SPHERES - 8)
                value = (
                    centres_ref[robot, axis, start_row : start_row + 8, 0:LANES] * weights[0]
                    + centres_ref[robot, axis, start_row : start_row + 8, LANES:COLUMNS] * weights[1]
                )
                if group == GROUPS - 1:
                    value = pltpu.roll(value, 4, 0)
                value = value + pltpu.roll(value, 64, 1)
                units[robot].append(value + pltpu.roll(value, 32, 1))
        units[robot].append(jnp.zeros((8, LANES), jnp.float32))
    for v in range(CHUNK):
        value = jnp.where(
            quarter < 2,
            jnp.where(quarter == 0, units[0][2 * v], units[0][2 * v + 1]),
            jnp.where(quarter == 2, units[1][2 * v], units[1][2 * v + 1]),
        )
        done = 0
        while done < 8:
            chunk, row = divmod(8 * v + done, CHUNK)
            length = min(8 - done, CHUNK - row)
            packed[chunk, row : row + length, :] = value[done : done + length, :]
            done += length
    for chunk in range(Z):
        packed[chunk, CHUNK : CHUNK + 1, :] = total_row

    copies = [
        start(packed.at[peer], parts.at[number], part_sems, number, (me, x * Z + peer))
        for number, peer in enumerate(z_peers)
    ]
    found = packed[z]
    for number, copy in enumerate(copies):
        copy.wait_recv()
        found = found + parts[number]
    sent = sent + copies

    mine[...] = found
    copy = start(mine, other, pair_sems, 0, (me, opposite))
    copy.wait_recv()
    sent = sent + [copy]
    found = mine[...] + other[...]
    gathered[z] = found / found[CHUNK : CHUNK + 1, :]

    copies = [
        start(gathered.at[z], gathered.at[z], gather_sems, number, (me, x * Z + peer))
        for number, peer in enumerate(z_peers)
    ]
    for copy in copies:
        copy.wait_recv()
    sent = sent + copies

    for chunk in range(Z):
        value = gathered[chunk]
        turned = [value] + [pltpu.roll(value, LANES - W * q, 1) for q in range(1, 4)]
        row = 0
        while row < CHUNK:
            v, at = divmod(CHUNK * chunk + row, 8)
            length = min(8 - at, CHUNK - row)
            for q in range(4):
                robot, unit = q // 2, 2 * v + q % 2
                if unit < 3 * GROUPS:
                    axis, group = divmod(unit, GROUPS)
                    first = 8 * group + at
                    rows = min(length, SPHERES - first)
                    if rows > 0:
                        blended_ref[robot, axis, first : first + rows, :] = turned[q][
                            row : row + rows, 0:W
                        ]
            row += length

    for copy in sent:
        copy.wait_send()


def in_vmem(count):
    return [pl.BlockSpec(memory_space=pltpu.VMEM)] * count


IN_SMEM = pl.BlockSpec(memory_space=pltpu.SMEM)


def local(centres, sphere_radius, counts, adjacency):
    dma = pltpu.SemaphoreType.DMA
    f32 = jnp.float32
    peers = ROBOT_DEVICES - 1
    received, self_cost, table = pl.pallas_call(
        spread_kernel,
        out_shape=(
            jax.ShapeDtypeStruct((ROBOT_DEVICES * ROWS, LANES), f32),
            jax.ShapeDtypeStruct((2 * ROBOTS_HERE, LANES), f32),
            jax.ShapeDtypeStruct((ROBOTS, LANES), jnp.int32),
        ),
        in_specs=[IN_SMEM] + in_vmem(3),
        out_specs=tuple(in_vmem(3)),
        scratch_shapes=[
            pltpu.VMEM((ROBOT_DEVICES * ROWS, LANES), f32),
            pltpu.VMEM((2 * ROBOTS_HERE, 4, 64, LANES), f32),
            pltpu.VMEM((ROBOTS_HERE, LANES), jnp.int32),
            pltpu.VMEM((ROBOT_DEVICES, ROBOTS_HERE, LANES), jnp.int32),
            pltpu.VMEM((ROBOTS, LANES), jnp.int32),
            dma((peers,)),
            dma((peers,)),
            dma((peers,)),
            dma((peers,)),
        ],
        compiler_params=pltpu.CompilerParams(collective_id=0, has_side_effects=True),
        name="spread",
    )(counts, centres, sphere_radius, adjacency)
    cost = pl.pallas_call(
        cross_kernel,
        out_shape=jax.ShapeDtypeStruct((ROBOT_DEVICES, ROBOTS_HERE, LANES), f32),
        in_specs=[IN_SMEM] + in_vmem(1),
        out_specs=in_vmem(1)[0],
        scratch_shapes=[
            pltpu.VMEM((ROBOTS, 4 * GROUPS, 8, LANES), f32),
            pltpu.VMEM((ROBOTS, 8, LANES), f32),
        ],
        name="cross",
    )(table, received)
    return pl.pallas_call(
        blend_kernel,
        out_shape=(
            jax.ShapeDtypeStruct((ROBOTS_HERE, COLUMNS), f32),
            jax.ShapeDtypeStruct((ROBOTS_HERE, 3, SPHERES, W), f32),
        ),
        in_specs=in_vmem(3),
        out_specs=tuple(in_vmem(2)),
        scratch_shapes=[
            pltpu.VMEM((ROBOT_DEVICES, ROBOTS_HERE, LANES), f32),
            pltpu.VMEM((2, ROBOTS_HERE, LANES), f32),
            pltpu.VMEM((Z, CHUNK + 1, LANES), f32),
            pltpu.VMEM((Z - 1, CHUNK + 1, LANES), f32),
            pltpu.VMEM((CHUNK + 1, LANES), f32),
            pltpu.VMEM((CHUNK + 1, LANES), f32),
            pltpu.VMEM((Z, CHUNK + 1, LANES), f32),
            dma((2, peers)),
            dma((2, Z - 1)),
            dma((2, 1)),
            dma((2, Z - 1)),
        ],
        compiler_params=pltpu.CompilerParams(collective_id=1, has_side_effects=True),
        name="blend",
    )(cost, self_cost, centres)


def solution(mesh):
    return jax.shard_map(
        local,
        mesh=mesh,
        in_specs=(P("robot", None, None, "seed"), P("robot", None), P("robot"), P("robot", None)),
        out_specs=(P("robot", "seed"), P("robot", None, None, None)),
        check_vma=False,
    )
```

time: 366 us -> 64.7 us (0.18); the launches traced: 359 us -> 64.8 us
  loops' own time: 130 us -> 0 us
  starting transfers between devices: 97 us -> 0 us
  Pallas kernels: 0 us -> 60.2 us
  local copies, waits for them, and re-layouts: 63.7 us -> 3.98 us
  blocking collectives: 26.5 us -> 0 us
  other arithmetic: 25.2 us -> 0 us
  waiting for transfers between devices: 15.4 us -> 0 us
    another operation x54 -> x0, loops' own time: 130 us -> none  [the longest x9 116 us: cross_costs(): lax.map(one_pair, jnp.arange(robots_here * arrived_count, dtype=jnp.int32))]
    ppermute x25 -> x0, starting transfers between devices: 97 us -> none  [shifted(): return lax.ppermute(block, axis, route)]
    pallas_call x0 -> x3, Pallas kernels: none -> 60.2 us  [the longest x1 27.5 us: local(): pl.pallas_call(blend_kernel, out_shape=(jax.ShapeDtypeStruct((ROBOTS_HERE...]
    dynamic_slice x88 -> x0, local copies, waits for them, and re-layouts: 55.1 us -> none  [the longest x36 23.1 us: one_pair(): link_rows[first_row, second_row] != 0]
    all_to_all x1 -> x0, blocking collectives: 26.5 us -> none  [sent_to_all(): return lax.all_to_all(copies, axis, split_axis=0, concat_axis=0, tiled=True)]
    reduce_sum x27 -> x0, other arithmetic: 19.4 us -> none  [the longest x14 18.4 us: tile_cost(): jnp.sum(weights[:, :, None] * jnp.exp(-distance / (spread * spread)), axi...]
    ppermute x25 -> x0, waiting for transfers between devices: 15.4 us -> none  [shifted(): return lax.ppermute(block, axis, route)]
  transfers between devices with their start and end apart: 25 -> 0, of which waited for: 8 -> 0; matrix products, arithmetic and copies ran while one was open for 19% -> 0% of each run, Pallas kernels for 0% -> 0%
where the time goes in v1:
time: 64.7 us; the launch traced here: 64.8 us
  Pallas kernels  60.2 us (93%)
  local copies, waits for them, and re-layouts  3.98 us (6%)
  between operations  0.65 us (1%)
    pallas_call x1, Pallas kernels, local(): pl.pallas_call(blend_kernel, out_shape=(jax.ShapeDtypeStruct((ROBOTS_HERE...  27.5 us
    pallas_call x1, Pallas kernels, local(): pl.pallas_call(cross_kernel, out_shape=jax.ShapeDtypeStruct((ROBOT_DEVICE...  19.2 us
    pallas_call x1, Pallas kernels, local(): pl.pallas_call(spread_kernel, out_shape=(jax.ShapeDtypeStruct((ROBOT_DEVI...  13.5 us
    unnamed x4, local copies, waits for them, and re-layouts  2.31 us
    pallas_call x1, local copies, waits for them, and re-layouts, local(): pl.pallas_call(blend_kernel, out_shape=(jax.ShapeDtypeStruct((ROBOTS_HERE...  1.67 us

profile of v1, /device:TPU:2, one launch (start us, length us, event | category | flops | bytes accessed | tf_op | source)
XLA Modules:
  0.0 64.8 jit_solution(2552010340345443789)
XLA Ops:
  0.6 1.7 %copy.6.centres_ref = f32[2,3,52,256]{3,2,1,0:T(8,128)} copy(f32[2,3,52,256]{3,0,2,1:T(2,128)} %param.4) | data formatting | bytes 638976 | tf_op args[0]
  2.4 13.5 %spread.1 = (f32[896,128]{1,0:T(8,128)}, f32[4,128]{1,0:T(4,128)}, s32[32,128]{1,0:T(8,128)}) custom-call(s32[2]{0:T(128)} %counts_ref.1, f32[2,3,52,256]{3,2,1,0:T(8,128)} %copy.6.centres_ref, f32[2,52]{1,0:T(2,128)} %radius_ref.1, s32[2,32]{1,0:T(2,128)} %adjacency_ref.1), custom_call_target="tpu_custom_call" | custom-call | tf_op jit(solution)/shard_map/spread/pallas_call | solution.py:424
  15.8 19.2 %cross.1.cost_ref = f32[16,2,128]{2,1,0:T(2,128)} custom-call(s32[32,128]{1,0:T(8,128)} %get-tuple-element.5.table, f32[896,128]{1,0:T(8,128)} %get-tuple-element.6.rows), custom_call_target="tpu_custom_call" | custom-call | tf_op jit(solution)/shard_map/cross/pallas_call | solution.py:447
  35.0 27.5 %blend.1 = (f32[2,256]{1,0:T(2,128)}, f32[2,3,52,32]{3,2,1,0:T(8,128)}) custom-call(f32[16,2,128]{2,1,0:T(2,128)} %cross.1.cost_ref, f32[4,128]{1,0:T(4,128)} %get-tuple-element.7.self_ref, f32[2,3,52,256]{3,2,1,0:T(8,128)} %copy.6.centres_ref), custom_call_target="tpu_custom_call" | custom-call | tf_op jit(solution)/shard_map/blend/pallas_call | solution.py:458
  62.6 0.0 copy-start
  62.6 1.7 %copy.8 = f32[2,3,52,32]{2,3,1,0:T(8,128)} copy(f32[2,3,52,32]{3,2,1,0:T(8,128)} %get-tuple-element.9) | data formatting | bytes 79872 | tf_op jit(solution)/shard_map/blend/pallas_call | solution.py:458
  64.2 0.0 copy-done
  64.2 0.6 copy.10
Async XLA Ops:
  62.6 1.7 %copy-start = (f32[2,256]{1,0:T(2,128)S(1)}, f32[2,256]{1,0:T(2,128)}, u32[]{:S(2)}) copy-start(f32[2,256]{1,0:T(2,128)} %get-tuple-element.12) | copy-start | bytes 6148

commit v2 on v1

--- a/solution.py
+++ b/solution.py
@@ -22,10 +22,14 @@
 Z = 8
 CHUNK = 11
 COUNT_LANE = 32
-LENGTH_LANE = 32
-GROUPS_LANE = 33
 ROOT = math.sqrt(math.log2(math.e))
 FAR = 1.0e6
+LIST = 256
+STEP_ROWS = 8
+ROW_IDS = ROBOTS * GROUPS
+STEPS_PLACE = LIST
+GROUPS_PLACE = LIST + 1
+GRANT = 16 * 1024 * 1024
 MESH = pl.DeviceIdType.MESH
 
 
@@ -37,6 +41,13 @@
     dx, dy, dz = a[0] - b[0], a[1] - b[1], a[2] - b[2]
     spread = a[3] + b[3]
     return jnp.exp2((dx * dx + dy * dy + dz * dz) / (-spread * spread))
+
+
+def centre_rows(ref, robot, axis, group, half):
+    first = min(8 * group, SPHERES - 8)
+    row = ((axis * SPHERES + first) * 2 + half) * ROBOTS_HERE + robot
+    value = ref[pl.ds(row, 8, stride=2 * ROBOTS_HERE), :]
+    return value if first == 8 * group else pltpu.roll(value, 4, 0)
 
 
 def spread_kernel(
@@ -84,15 +95,9 @@
             active = sphere < count
             far = FAR * (sphere + number).astype(jnp.float32)
             for half in range(2):
-                at = slice(half * LANES, (half + 1) * LANES)
                 out, square = [], None
                 for axis in range(3):
-                    if group < GROUPS - 1:
-                        here = centres_ref[robot, axis, 8 * group : 8 * group + 8, at]
-                    else:
-                        here = pltpu.roll(
-                            centres_ref[robot, axis, SPHERES - 8 : SPHERES, at], 4, 0
-                        )
+                    here = centre_rows(centres_ref, robot, axis, group, half)
                     ahead = jnp.where(last_waypoint, here, pltpu.roll(here, LANES - 1, 1))
                     step = ahead - here
                     square = step * step if square is None else square + step * step
@@ -177,17 +182,27 @@
     noted = note[...].astype(jnp.float32)
     link = jnp.where((column > row) & (column < ROBOTS) & (noted != 0.0), 1.0, 0.0)
     counts = jnp.sum(jnp.where(column == COUNT_LANE, noted, 0.0), axis=1, keepdims=True)
+    groups = jnp.floor((counts + 7.0) * 0.125)
+    groups_row = jnp.sum(jnp.where(row == column, groups, 0.0), axis=0, keepdims=True)
+    length = link * groups_row
     before = (iota(0, (LANES, LANES)) < iota(1, (LANES, LANES))).astype(jnp.float32)
-    rank = jnp.dot(link, before, preferred_element_type=jnp.float32)
-    linked_column = link * column.astype(jnp.float32)
-    table = jnp.zeros(shape, jnp.float32)
-    for place in range(ROBOTS - 1):
-        found = jnp.sum(jnp.where(rank == float(place), linked_column, 0.0), axis=1, keepdims=True)
-        table = jnp.where(column == place, found, table)
-    table = jnp.where(column == LENGTH_LANE, jnp.sum(link, axis=1, keepdims=True), table)
-    table = table.astype(jnp.int32)
-    groups = (counts.astype(jnp.int32) + 7) >> 3
-    table_ref[...] = jnp.where(column == GROUPS_LANE, groups, table)
+    start = jnp.dot(length, before, preferred_element_type=jnp.float32)
+    end = start + length
+    place = iota(1, (ROBOTS, LIST)).astype(jnp.float32)
+    rows_listed = jnp.full((ROBOTS, LIST), float(ROW_IDS))
+    for robot in range(1, ROBOTS):
+        first, past = start[:, robot : robot + 1], end[:, robot : robot + 1]
+        rows_listed = jnp.where(
+            (place >= first) & (place < past), place + (float(GROUPS * robot) - first), rows_listed
+        )
+    steps = jnp.floor((jnp.sum(length, axis=1, keepdims=True) + (STEP_ROWS - 1.0)) * (1.0 / STEP_ROWS))
+    table_ref[:, 0:LIST] = rows_listed.astype(jnp.int32)
+    tail = jnp.where(column == 0, steps, groups)
+    table_ref[:, LIST : LIST + LANES] = tail.astype(jnp.int32)
+    filling = iota(0)
+    recv_ref[ROBOT_DEVICES * ROWS : ROBOT_DEVICES * ROWS + 8, :] = jnp.where(
+        filling == 0, -1000.0 * FAR, jnp.where(filling == 3, 1.0, 0.0)
+    )
 
     for copy in copies:
         copy.wait_recv()
@@ -196,60 +211,63 @@
 
 
 def cross_kernel(table, rows, cost_ref, turned, total):
-    def prepare(robot, carry):
-        for row in range(4 * GROUPS):
-            line = rows[pl.ds(robot * (4 * GROUPS) + row, 1), :]
-            turned[robot, row] = pltpu.roll(
-                jnp.broadcast_to(line, (8, LANES)), 0, 1, stride=PART, stride_axis=0
-            )
-        total[robot] = jnp.zeros((8, LANES), jnp.float32)
+    def prepare(index, carry):
+        for part in range(4):
+            robot = index * 4 + part
+            for row in range(4 * GROUPS):
+                line = rows[pl.ds(robot * (4 * GROUPS) + row, 1), :]
+                turned[robot, row] = pltpu.roll(
+                    jnp.broadcast_to(line, (8, LANES)), 0, 1, stride=PART, stride_axis=0
+                )
+            for group in range(GROUPS):
+                total[robot * GROUPS + group] = jnp.zeros((8, LANES), jnp.float32)
         return carry
 
-    lax.fori_loop(0, ROBOTS, prepare, 0)
-
-    def pair_sum(first_groups, second_groups, first, second):
-        sums = [None] * 4
-        turn = 0
-        for second_group in range(second_groups):
-            b = [
-                jnp.broadcast_to(
-                    rows[pl.ds(second * (4 * GROUPS) + second_group * 4 + q, 1), :], (8, LANES)
+    lax.fori_loop(0, ROBOTS // 4, prepare, 0)
+
+    def of_robot(first, carry):
+        first_groups = table[first, GROUPS_PLACE]
+
+        for known_groups in range(FIRST_GROUPS, GROUPS + 1):
+
+            @pl.when(first_groups == known_groups)
+            def _():
+                def of_rows(step, own):
+                    ids = [table[first, step * STEP_ROWS + n] for n in range(STEP_ROWS)]
+                    olds = [total[row_id] for row_id in ids]
+                    news = []
+                    for row_id in ids:
+                        b = [
+                            jnp.broadcast_to(rows[pl.ds(row_id * 4 + q, 1), :], (8, LANES))
+                            for q in range(4)
+                        ]
+                        found = None
+                        for group in range(known_groups):
+                            a = [turned[first, group * 4 + q] for q in range(4)]
+                            term = pair_term(a, b)
+                            found = term if found is None else found + term
+                        news.append(found)
+                    for row_id, old, new in zip(ids, olds, news):
+                        total[row_id] = old + new
+                    while len(news) > 1:
+                        news = [m + n for m, n in zip(news[0::2], news[1::2])]
+                    return own + news[0]
+
+                own = lax.fori_loop(
+                    0, table[first, STEPS_PLACE], of_rows, jnp.zeros((8, LANES), jnp.float32)
                 )
-                for q in range(4)
-            ]
-            for first_group in range(first_groups):
-                a = [turned[first, first_group * 4 + q] for q in range(4)]
-                term = pair_term(a, b)
-                sums[turn] = term if sums[turn] is None else sums[turn] + term
-                turn = (turn + 1) % 4
-        return (sums[0] + sums[1]) + (sums[2] + sums[3])
-
-    def of_robot(first, carry):
-        first_groups = table[first, GROUPS_LANE]
-
-        def of_pair(place, carry):
-            second = table[first, place]
-            second_groups = table[second, GROUPS_LANE]
-            case = (first_groups - FIRST_GROUPS) * 4 + (second_groups - FIRST_GROUPS)
-            found = lax.switch(
-                case,
-                [
-                    functools.partial(pair_sum, m, n)
-                    for m in range(FIRST_GROUPS, GROUPS + 1)
-                    for n in range(FIRST_GROUPS, GROUPS + 1)
-                ],
-                first,
-                second,
-            )
-            total[first] = total[first] + found
-            total[second] = total[second] + found
-            return carry
-
-        return lax.fori_loop(0, table[first, LENGTH_LANE], of_pair, carry)
+                total[first * GROUPS] = total[first * GROUPS] + own
+
+        return carry
 
     lax.fori_loop(0, ROBOTS, of_robot, 0)
 
-    cost = jnp.sum(total[...], axis=1)
+    for robot in range(ROBOTS):
+        found = total[robot * GROUPS]
+        for group in range(1, GROUPS):
+            found = found + total[robot * GROUPS + group]
+        turned[robot, 0] = found
+    cost = jnp.sum(turned[:, 0], axis=1)
     for shift in (64, 32, 16):
         cost = cost + pltpu.roll(cost, shift, 1)
     cost = cost * (1.0 / (SPHERES * SPHERES))
@@ -262,14 +280,13 @@
     self_ref,
     centres_ref,
     robot_cost_ref,
-    blended_ref,
+    gathered,
     cost_recv,
     weight,
     packed,
     parts,
     mine,
     other,
-    gathered,
     cost_sems,
     part_sems,
     pair_sems,
@@ -337,21 +354,18 @@
         ]
         for axis in range(3):
             for group in range(GROUPS):
-                start_row = min(8 * group, SPHERES - 8)
                 value = (
-                    centres_ref[robot, axis, start_row : start_row + 8, 0:LANES] * weights[0]
-                    + centres_ref[robot, axis, start_row : start_row + 8, LANES:COLUMNS] * weights[1]
+                    centre_rows(centres_ref, robot, axis, group, 0) * weights[0]
+                    + centre_rows(centres_ref, robot, axis, group, 1) * weights[1]
                 )
-                if group == GROUPS - 1:
-                    value = pltpu.roll(value, 4, 0)
                 value = value + pltpu.roll(value, 64, 1)
                 units[robot].append(value + pltpu.roll(value, 32, 1))
         units[robot].append(jnp.zeros((8, LANES), jnp.float32))
     for v in range(CHUNK):
         value = jnp.where(
             quarter < 2,
-            jnp.where(quarter == 0, units[0][2 * v], units[0][2 * v + 1]),
-            jnp.where(quarter == 2, units[1][2 * v], units[1][2 * v + 1]),
+            jnp.where(quarter == 0, units[0][v], units[0][CHUNK + v]),
+            jnp.where(quarter == 2, units[1][v], units[1][CHUNK + v]),
         )
         done = 0
         while done < 8:
@@ -387,27 +401,28 @@
         copy.wait_recv()
     sent = sent + copies
 
-    for chunk in range(Z):
-        value = gathered[chunk]
-        turned = [value] + [pltpu.roll(value, LANES - W * q, 1) for q in range(1, 4)]
-        row = 0
-        while row < CHUNK:
-            v, at = divmod(CHUNK * chunk + row, 8)
-            length = min(8 - at, CHUNK - row)
-            for q in range(4):
-                robot, unit = q // 2, 2 * v + q % 2
-                if unit < 3 * GROUPS:
-                    axis, group = divmod(unit, GROUPS)
-                    first = 8 * group + at
-                    rows = min(length, SPHERES - first)
-                    if rows > 0:
-                        blended_ref[robot, axis, first : first + rows, :] = turned[q][
-                            row : row + rows, 0:W
-                        ]
-            row += length
-
     for copy in sent:
         copy.wait_send()
+
+
+def finish_kernel(cost_in, gathered, cost_out, blended, lines):
+    cost_out[...] = cost_in[...]
+    for chunk in range(Z):
+        lines[CHUNK * chunk : CHUNK * (chunk + 1), :] = gathered[chunk, 0:CHUNK, :]
+    turned = lines[...].T
+    for robot in range(ROBOTS_HERE):
+        for axis in range(3):
+            for quarter in range(2):
+                low = max(axis * GROUPS, quarter * CHUNK)
+                high = min((axis + 1) * GROUPS, (quarter + 1) * CHUNK)
+                if low < high:
+                    source = (robot * 2 + quarter) * W
+                    lane = 8 * (low - quarter * CHUNK)
+                    first = 8 * (low - axis * GROUPS)
+                    width = min(8 * (high - low), SPHERES - first)
+                    blended[robot, axis, :, first : first + width] = turned[
+                        source : source + W, lane : lane + width
+                    ]
 
 
 def in_vmem(count):
@@ -421,12 +436,14 @@
     dma = pltpu.SemaphoreType.DMA
     f32 = jnp.float32
     peers = ROBOT_DEVICES - 1
+    rows = centres.transpose(1, 2, 0, 3).reshape(3 * SPHERES, ROBOTS_HERE, 2, LANES)
+    rows = rows.transpose(0, 2, 1, 3).reshape(3 * SPHERES * 2 * ROBOTS_HERE, LANES)
     received, self_cost, table = pl.pallas_call(
         spread_kernel,
         out_shape=(
-            jax.ShapeDtypeStruct((ROBOT_DEVICES * ROWS, LANES), f32),
+            jax.ShapeDtypeStruct((ROBOT_DEVICES * ROWS + 8, LANES), f32),
             jax.ShapeDtypeStruct((2 * ROBOTS_HERE, LANES), f32),
-            jax.ShapeDtypeStruct((ROBOTS, LANES), jnp.int32),
+            jax.ShapeDtypeStruct((ROBOTS, LIST + LANES), jnp.int32),
         ),
         in_specs=[IN_SMEM] + in_vmem(3),
         out_specs=tuple(in_vmem(3)),
@@ -441,9 +458,11 @@
             dma((peers,)),
             dma((peers,)),
         ],
-        compiler_params=pltpu.CompilerParams(collective_id=0, has_side_effects=True),
+        compiler_params=pltpu.CompilerParams(
+            collective_id=0, has_side_effects=True, vmem_limit_bytes=GRANT
+        ),
         name="spread",
-    )(counts, centres, sphere_radius, adjacency)
+    )(counts, rows, sphere_radius, adjacency)
     cost = pl.pallas_call(
         cross_kernel,
         out_shape=jax.ShapeDtypeStruct((ROBOT_DEVICES, ROBOTS_HERE, LANES), f32),
@@ -451,15 +470,16 @@
         out_specs=in_vmem(1)[0],
         scratch_shapes=[
             pltpu.VMEM((ROBOTS, 4 * GROUPS, 8, LANES), f32),
-            pltpu.VMEM((ROBOTS, 8, LANES), f32),
+            pltpu.VMEM((ROW_IDS + 1, 8, LANES), f32),
         ],
+        compiler_params=pltpu.CompilerParams(vmem_limit_bytes=GRANT),
         name="cross",
     )(table, received)
-    return pl.pallas_call(
+    robot_cost, gathered = pl.pallas_call(
         blend_kernel,
         out_shape=(
             jax.ShapeDtypeStruct((ROBOTS_HERE, COLUMNS), f32),
-            jax.ShapeDtypeStruct((ROBOTS_HERE, 3, SPHERES, W), f32),
+            jax.ShapeDtypeStruct((Z, CHUNK + 1, LANES), f32),
         ),
         in_specs=in_vmem(3),
         out_specs=tuple(in_vmem(2)),
@@ -470,15 +490,29 @@
             pltpu.VMEM((Z - 1, CHUNK + 1, LANES), f32),
             pltpu.VMEM((CHUNK + 1, LANES), f32),
             pltpu.VMEM((CHUNK + 1, LANES), f32),
-            pltpu.VMEM((Z, CHUNK + 1, LANES), f32),
             dma((2, peers)),
             dma((2, Z - 1)),
             dma((2, 1)),
             dma((2, Z - 1)),
         ],
-        compiler_params=pltpu.CompilerParams(collective_id=1, has_side_effects=True),
+        compiler_params=pltpu.CompilerParams(
+            collective_id=1, has_side_effects=True, vmem_limit_bytes=GRANT
+        ),
         name="blend",
-    )(cost, self_cost, centres)
+    )(cost, self_cost, rows)
+    robot_cost, blended = pl.pallas_call(
+        finish_kernel,
+        out_shape=(
+            jax.ShapeDtypeStruct((ROBOTS_HERE, COLUMNS), f32),
+            jax.ShapeDtypeStruct((ROBOTS_HERE, 3, W, SPHERES), f32),
+        ),
+        in_specs=in_vmem(2),
+        out_specs=tuple(in_vmem(2)),
+        scratch_shapes=[pltpu.VMEM((LANES, LANES), f32)],
+        compiler_params=pltpu.CompilerParams(vmem_limit_bytes=GRANT),
+        name="finish",
+    )(robot_cost, gathered)
+    return robot_cost, blended.transpose(0, 1, 3, 2)
 
 
 def solution(mesh):

time: 64.7 us -> 56.3 us (0.87); the launches traced: 64.8 us -> 55.2 us
  Pallas kernels: 60.2 us -> 52.2 us
  local copies, waits for them, and re-layouts: 3.98 us -> 2.33 us
    pallas_call x1, Pallas kernels: 19.2 us -> 13 us  [local(): pl.pallas_call(cross_kernel, out_shape=jax.ShapeDtypeStruct((ROBOT_DEVICE...]
    pallas_call x1 -> x0, local copies, waits for them, and re-layouts: 1.67 us -> none  [local(): pl.pallas_call(blend_kernel, out_shape=(jax.ShapeDtypeStruct((ROBOTS_HERE...]
    pallas_call x1, Pallas kernels: 27.5 us -> 26.2 us  [local(): pl.pallas_call(blend_kernel, out_shape=(jax.ShapeDtypeStruct((ROBOTS_HERE...]
    pallas_call x1, Pallas kernels: 13.5 us -> 12.2 us  [local(): pl.pallas_call(spread_kernel, out_shape=(jax.ShapeDtypeStruct((ROBOT_DEVI...]
    pallas_call x0 -> x1, Pallas kernels: none -> 0.83 us  [local(): pl.pallas_call(finish_kernel, out_shape=(jax.ShapeDtypeStruct((ROBOTS_HER...]
    unnamed x4 -> x10, local copies, waits for them, and re-layouts: 2.31 us -> 2.33 us
where the time goes in v2:
time: 56.3 us; the launch traced here: 55.2 us
  Pallas kernels  52.2 us (93%)
  local copies, waits for them, and re-layouts  2.33 us (4%)
  between operations  0.67 us (1%)
    pallas_call x1, Pallas kernels, local(): pl.pallas_call(blend_kernel, out_shape=(jax.ShapeDtypeStruct((ROBOTS_HERE...  26.2 us
    pallas_call x1, Pallas kernels, local(): pl.pallas_call(cross_kernel, out_shape=jax.ShapeDtypeStruct((ROBOT_DEVICE...  13 us
    pallas_call x1, Pallas kernels, local(): pl.pallas_call(spread_kernel, out_shape=(jax.ShapeDtypeStruct((ROBOT_DEVI...  12.2 us
    unnamed x10, local copies, waits for them, and re-layouts  2.33 us

profile of v2, /device:TPU:2, one launch (start us, length us, event | category | flops | bytes accessed | tf_op | source)
XLA Modules:
  0.0 55.2 jit_solution(17770172658565604433)
XLA Ops:
  0.6 0.0 copy-start.4
  0.6 0.0 copy-start.2
  0.7 0.6 %copy-done.4 = s32[2]{0:T(128)S(1)} copy-done((s32[2]{0:T(128)S(1)}, s32[2]{0:T(128)}, u32[]{:S(2)}) %copy-start.4) | copy-done | bytes 32
  1.3 0.0 copy-done.2
  1.3 0.0 copy-start
  1.3 1.0 %copy-done = f32[2,3,52,256]{3,0,2,1:T(2,128)S(1)} copy-done((f32[2,3,52,256]{3,0,2,1:T(2,128)S(1)}, f32[2,3,52,256]{3,0,2,1:T(2,128)}, u32[]{:S(2)}) %copy-start) | copy-done | bytes 319512
  2.3 0.0 copy-start.3
  2.3 0.7 %copy-done.3 = s32[2,32]{1,0:T(2,128)S(1)} copy-done((s32[2,32]{1,0:T(2,128)S(1)}, s32[2,32]{1,0:T(2,128)}, u32[]{:S(2)}) %copy-start.3) | copy-done | bytes 280
  3.0 12.2 %spread.1 = (f32[904,128]{1,0:T(8,128)S(1)}, f32[4,128]{1,0:T(4,128)S(1)}, s32[32,384]{1,0:T(8,128)S(1)}) custom-call(s32[2]{0:T(128)S(1)} %copy-done.4, f32[624,128]{1,0:T(8,128)S(1)} %bitcast.8, f32[2,52]{1,0:T(2,128)S(1)} %copy-done.2, s32[2,32]{1,0:T(2,128)S(1)} %copy-done.3), custom_call_target="tpu_custom_call" | custom-call | tf_op jit(solution)/shard_map/spread/pallas_call | solution.py:441
  15.2 0.0 copy-start.1
  15.2 13.0 %cross.1.cost_ref = f32[16,2,128]{2,1,0:T(2,128)S(1)} custom-call(s32[32,384]{1,0:T(8,128)S(1)} %get-tuple-element.9.table, f32[904,128]{1,0:T(8,128)S(1)} %get-tuple-element.10.rows), custom_call_target="tpu_custom_call" | custom-call | tf_op jit(solution)/shard_map/cross/pallas_call | solution.py:466
  28.2 0.0 copy-done.1
  28.2 26.2 %blend.1 = (f32[2,256]{1,0:T(2,128)S(1)}, f32[8,12,128]{2,1,0:T(8,128)S(1)}) custom-call(f32[16,2,128]{2,1,0:T(2,128)S(1)} %cross.1.cost_ref, f32[4,128]{1,0:T(4,128)S(1)} %get-tuple-element.11.self_ref, f32[624,128]{1,0:T(8,128)S(1)} %bitcast.9), custom_call_target="tpu_custom_call" | custom-call | tf_op jit(solution)/shard_map/blend/pallas_call | solution.py:478
  54.4 0.8 %finish.1 = (f32[2,256]{1,0:T(2,128)}, f32[2,3,32,52]{3,2,1,0:T(8,128)}) custom-call(f32[2,256]{1,0:T(2,128)S(1)} %get-tuple-element.12.cost_in, f32[8,12,128]{2,1,0:T(8,128)S(1)} %get-tuple-element.13.gathered), custom_call_target="tpu_custom_call" | custom-call | tf_op jit(solution)/shard_map/finish/pallas_call | solution.py:503
Async XLA Ops:
  0.6 0.7 %copy-start.4 = (s32[2]{0:T(128)S(1)}, s32[2]{0:T(128)}, u32[]{:S(2)}) copy-start(s32[2]{0:T(128)} %counts_ref.1) | copy-start | bytes 28
  0.6 0.7 %copy-start.2 = (f32[2,52]{1,0:T(2,128)S(1)}, f32[2,52]{1,0:T(2,128)}, u32[]{:S(2)}) copy-start(f32[2,52]{1,0:T(2,128)} %radius_ref.1) | copy-start | bytes 1252
  1.3 1.0 %copy-start = (f32[2,3,52,256]{3,0,2,1:T(2,128)S(1)}, f32[2,3,52,256]{3,0,2,1:T(2,128)}, u32[]{:S(2)}) copy-start(f32[2,3,52,256]{3,0,2,1:T(2,128)} %param.4) | copy-start | bytes 958468
  2.3 0.7 %copy-start.3 = (s32[2,32]{1,0:T(2,128)S(1)}, s32[2,32]{1,0:T(2,128)}, u32[]{:S(2)}) copy-start(s32[2,32]{1,0:T(2,128)} %adjacency_ref.1) | copy-start | bytes 772
  15.2 13.0 %copy-start.1 = (f32[2,3,52,256]{3,0,2,1:T(2,128)S(1)}, f32[2,3,52,256]{3,0,2,1:T(2,128)}, u32[]{:S(2)}) copy-start(f32[2,3,52,256]{3,0,2,1:T(2,128)} %param.4) | copy-start | bytes 958468

commit v3 on v2

--- a/solution.py
+++ b/solution.py
@@ -24,11 +24,16 @@
 COUNT_LANE = 32
 ROOT = math.sqrt(math.log2(math.e))
 FAR = 1.0e6
-LIST = 256
 STEP_ROWS = 8
 ROW_IDS = ROBOTS * GROUPS
-STEPS_PLACE = LIST
-GROUPS_PLACE = LIST + 1
+WORDS = 56
+STEPS_WORD = 56
+ENTRY = 64
+ORDER = ROBOTS * ENTRY
+CASE_STEPS = ORDER + 32
+CASE_START = ORDER + 40
+TABLE_ROWS = 24
+EARLY_GROUPS = 3
 GRANT = 16 * 1024 * 1024
 MESH = pl.DeviceIdType.MESH
 
@@ -37,10 +42,14 @@
     return lax.broadcasted_iota(jnp.int32, shape, axis)
 
 
-def pair_term(a, b):
+def pair_argument(a, b):
     dx, dy, dz = a[0] - b[0], a[1] - b[1], a[2] - b[2]
     spread = a[3] + b[3]
-    return jnp.exp2((dx * dx + dy * dy + dz * dz) / (-spread * spread))
+    return (dx * dx + dy * dy + dz * dz) / (-spread * spread)
+
+
+def pair_term(a, b):
+    return jnp.exp2(pair_argument(a, b))
 
 
 def centre_rows(ref, robot, axis, group, half):
@@ -51,18 +60,24 @@
 
 
 def spread_kernel(
+    counts_hbm,
+    centres_hbm,
+    radius_hbm,
+    adjacency_hbm,
+    recv_ref,
+    turned_ref,
+    self_ref,
+    table_ref,
     counts_ref,
     centres_ref,
     radius_ref,
     adjacency_ref,
-    recv_ref,
-    self_ref,
-    table_ref,
     send,
     swept,
     note_send,
     note_recv,
     note,
+    load_sem,
     send_sem,
     recv_sem,
     note_send_sem,
@@ -76,16 +91,40 @@
     for peer in peers:
         pl.semaphore_signal(barrier, inc=1, device_id=(peer, seed), device_id_type=MESH)
 
+    loads = [
+        pltpu.make_async_copy(counts_hbm, counts_ref, load_sem.at[0]),
+        pltpu.make_async_copy(radius_hbm, radius_ref, load_sem.at[1]),
+        pltpu.make_async_copy(adjacency_hbm, adjacency_ref, load_sem.at[2]),
+    ]
+    per_axis, early = 4 * SPHERES, 4 * 8 * EARLY_GROUPS
+    for axis in range(3):
+        at = pl.ds(axis * per_axis, early)
+        loads.append(pltpu.make_async_copy(centres_hbm.at[at], centres_ref.at[at], load_sem.at[3 + axis]))
+    for axis in range(3):
+        at = pl.ds(axis * per_axis + early, per_axis - early)
+        loads.append(pltpu.make_async_copy(centres_hbm.at[at], centres_ref.at[at], load_sem.at[6 + axis]))
+    for load in loads:
+        load.start()
+    for load in loads[:6]:
+        load.wait()
+
     sub, lane = iota(0), iota(1)
     part = lane // PART
     last_waypoint = lane % W == W - 1
     radius_lane = iota(1, (8, SPHERES))
     radius_sub = iota(0, (8, SPHERES))
+    note_send[...] = jnp.zeros((ROBOTS_HERE, LANES), jnp.int32)
+    note_send[:, 0:ROBOTS] = adjacency_ref[...]
     for robot in range(ROBOTS_HERE):
-        count = counts_ref[robot]
-        radius_row = jnp.broadcast_to(radius_ref[robot : robot + 1, :], (8, SPHERES))
-        number = (me * ROBOTS_HERE + robot) * 64 + 1
-        for group in range(GROUPS):
+        note_send[robot : robot + 1, COUNT_LANE : COUNT_LANE + 1] = jnp.full((1, 1), counts_ref[robot], jnp.int32)
+    for group in range(GROUPS):
+        if group == EARLY_GROUPS:
+            for load in loads[6:]:
+                load.wait()
+        for robot in range(ROBOTS_HERE):
+            count = counts_ref[robot]
+            radius_row = jnp.broadcast_to(radius_ref[robot : robot + 1, :], (8, SPHERES))
+            number = (me * ROBOTS_HERE + robot) * 64 + 1
             radius = jnp.sum(
                 jnp.where(radius_lane == radius_sub + 8 * group, radius_row, 0.0),
                 axis=1,
@@ -112,15 +151,6 @@
                         value = jnp.where(part & bit != 0, pltpu.roll(value, 8 - bit, 0), value)
                     row = (robot * GROUPS + group) * 4 + quantity
                     send[pl.ds(half * 8 * ROWS + row, 8, stride=ROWS), :] = value
-        for half in range(2):
-            for quantity in range(4):
-                fill = FAR * (sub + 56 + number).astype(jnp.float32) if quantity == 0 else jnp.full((8, LANES), float(quantity == 3))
-                swept[half * ROBOTS_HERE + robot, quantity, 56:64, :] = fill
-
-    note_send[...] = jnp.zeros((ROBOTS_HERE, LANES), jnp.int32)
-    note_send[:, 0:ROBOTS] = adjacency_ref[...]
-    for robot in range(ROBOTS_HERE):
-        note_send[robot : robot + 1, COUNT_LANE : COUNT_LANE + 1] = jnp.full((1, 1), counts_ref[robot], jnp.int32)
 
     pl.semaphore_wait(barrier, ROBOT_DEVICES - 1)
 
@@ -142,7 +172,6 @@
         )
         copy.start()
         notes.append(copy)
-    for number, peer in enumerate(peers):
         copy = pltpu.make_async_remote_copy(
             src_ref=send.at[rows_of(slot_of(peer))],
             dst_ref=recv_ref.at[rows_of(me)],
@@ -156,8 +185,27 @@
     note_recv[me] = note_send[...]
     recv_ref[rows_of(me), :] = send[rows_of(slot_of(me)), :]
 
+    def turn_rows(device):
+        def turn_group(index, carry):
+            row = pl.multiple_of(device * ROWS + index * 8, 8)
+            for n in range(8):
+                line = jnp.broadcast_to(recv_ref[pl.ds(row + n, 1), :], (8, LANES))
+                turned_ref[row + n] = pltpu.roll(line, 0, 1, stride=PART, stride_axis=0)
+            return carry
+
+        lax.fori_loop(0, ROWS // 8, turn_group, 0)
+
+    turn_rows(me)
+    for index in range(2 * ROBOTS_HERE):
+        robot = index % ROBOTS_HERE
+        number = (me * ROBOTS_HERE + robot) * 64 + 1
+        for quantity in range(4):
+            fill = jnp.full((8, LANES), float(quantity == 3))
+            if quantity == 0:
+                fill = FAR * (sub + 8 * GROUPS + number).astype(jnp.float32)
+            swept[index, quantity, 8 * GROUPS : 8 * GROUPS + 8, :] = fill
+
     def self_pairs(index, carry):
-        half, robot = index // ROBOTS_HERE, lax.rem(index, ROBOTS_HERE)
         sums = [jnp.zeros((8, LANES), jnp.float32) for _ in range(4)]
         turn = 0
         for group in range(GROUPS):
@@ -179,108 +227,133 @@
         note[ROBOTS_HERE * device : ROBOTS_HERE * (device + 1), :] = note_recv[device]
     shape = (ROBOTS, LANES)
     row, column = iota(0, shape), iota(1, shape)
+    row_number = row.astype(jnp.float32)
     noted = note[...].astype(jnp.float32)
     link = jnp.where((column > row) & (column < ROBOTS) & (noted != 0.0), 1.0, 0.0)
     counts = jnp.sum(jnp.where(column == COUNT_LANE, noted, 0.0), axis=1, keepdims=True)
     groups = jnp.floor((counts + 7.0) * 0.125)
-    groups_row = jnp.sum(jnp.where(row == column, groups, 0.0), axis=0, keepdims=True)
-    length = link * groups_row
+
+    def as_row(value):
+        return jnp.sum(jnp.where(row == column, value, 0.0), axis=0, keepdims=True)
+
+    length = link * as_row(groups)
     before = (iota(0, (LANES, LANES)) < iota(1, (LANES, LANES))).astype(jnp.float32)
     start = jnp.dot(length, before, preferred_element_type=jnp.float32)
     end = start + length
-    place = iota(1, (ROBOTS, LIST)).astype(jnp.float32)
-    rows_listed = jnp.full((ROBOTS, LIST), float(ROW_IDS))
-    for robot in range(1, ROBOTS):
-        first, past = start[:, robot : robot + 1], end[:, robot : robot + 1]
-        rows_listed = jnp.where(
-            (place >= first) & (place < past), place + (float(GROUPS * robot) - first), rows_listed
-        )
+    words = jnp.zeros(shape, jnp.int32)
+    for byte in range(4):
+        place = (column * 4 + byte).astype(jnp.float32)
+        listed = jnp.full(shape, float(ROW_IDS))
+        for robot in range(1, ROBOTS):
+            first, past = start[:, robot : robot + 1], end[:, robot : robot + 1]
+            listed = jnp.where(
+                (place >= first) & (place < past), place + (float(GROUPS * robot) - first), listed
+            )
+        words = words | (listed.astype(jnp.int32) << (8 * byte))
     steps = jnp.floor((jnp.sum(length, axis=1, keepdims=True) + (STEP_ROWS - 1.0)) * (1.0 / STEP_ROWS))
-    table_ref[:, 0:LIST] = rows_listed.astype(jnp.int32)
-    tail = jnp.where(column == 0, steps, groups)
-    table_ref[:, LIST : LIST + LANES] = tail.astype(jnp.int32)
-    filling = iota(0)
+    words = jnp.where(column == STEPS_WORD, steps.astype(jnp.int32), words)
+    note[...] = jnp.where(column < ENTRY, words, 0)
+    table_ref[0:16, :] = note[pl.ds(0, 16, stride=2), :] + pltpu.roll(
+        note[pl.ds(1, 16, stride=2), :], ENTRY, 1
+    )
+    busy = jnp.where(steps > 0.0, 1.0, 0.0)
+    key = groups * 32.0 + row_number
+    key_row, busy_row = as_row(key), as_row(busy)
+    rank = jnp.sum(jnp.where(key_row < key, busy_row, 0.0), axis=1, keepdims=True)
+    lane_number = column.astype(jnp.float32)
+    last = jnp.sum(
+        jnp.where((rank == lane_number) & (busy > 0.0), row_number, 0.0), axis=0, keepdims=True
+    )
+    line = iota(1, (1, LANES))
+    for case in range(FIRST_GROUPS, GROUPS + 1):
+        of_case = jnp.where(row == column, jnp.where(groups == float(case), steps, 0.0), 0.0)
+        earlier = jnp.where(row == column, jnp.where(groups < float(case), busy, 0.0), 0.0)
+        last = jnp.where(line == CASE_STEPS - ORDER + case - FIRST_GROUPS, jnp.sum(of_case), last)
+        last = jnp.where(line == CASE_START - ORDER + case - FIRST_GROUPS, jnp.sum(earlier), last)
+    table_ref[16:24, :] = jnp.broadcast_to(last, (8, LANES)).astype(jnp.int32)
     recv_ref[ROBOT_DEVICES * ROWS : ROBOT_DEVICES * ROWS + 8, :] = jnp.where(
-        filling == 0, -1000.0 * FAR, jnp.where(filling == 3, 1.0, 0.0)
+        sub == 0, -1000.0 * FAR, jnp.where(sub == 3, 1.0, 0.0)
     )
 
-    for copy in copies:
+    for number, copy in enumerate(copies):
         copy.wait_recv()
+        turn_rows(lax.rem(me + ROBOT_DEVICES - 1 - number, ROBOT_DEVICES))
     for copy in notes + copies:
         copy.wait_send()
 
 
-def cross_kernel(table, rows, cost_ref, turned, total):
-    def prepare(index, carry):
-        for part in range(4):
-            robot = index * 4 + part
-            for row in range(4 * GROUPS):
-                line = rows[pl.ds(robot * (4 * GROUPS) + row, 1), :]
-                turned[robot, row] = pltpu.roll(
-                    jnp.broadcast_to(line, (8, LANES)), 0, 1, stride=PART, stride_axis=0
-                )
-            for group in range(GROUPS):
-                total[robot * GROUPS + group] = jnp.zeros((8, LANES), jnp.float32)
+def cross_kernel(table, rows, turned, total, arguments):
+    zero = jnp.zeros((8, LANES), jnp.float32)
+    for slot in range(STEP_ROWS * GROUPS):
+        arguments[slot] = zero
+
+    def clear(index, carry):
+        for n in range(15):
+            total[index * 15 + n] = zero
         return carry
 
-    lax.fori_loop(0, ROBOTS // 4, prepare, 0)
-
-    def of_robot(first, carry):
-        first_groups = table[first, GROUPS_PLACE]
-
-        for known_groups in range(FIRST_GROUPS, GROUPS + 1):
-
-            @pl.when(first_groups == known_groups)
-            def _():
-                def of_rows(step, own):
-                    ids = [table[first, step * STEP_ROWS + n] for n in range(STEP_ROWS)]
-                    olds = [total[row_id] for row_id in ids]
-                    news = []
-                    for row_id in ids:
-                        b = [
-                            jnp.broadcast_to(rows[pl.ds(row_id * 4 + q, 1), :], (8, LANES))
-                            for q in range(4)
-                        ]
-                        found = None
-                        for group in range(known_groups):
-                            a = [turned[first, group * 4 + q] for q in range(4)]
-                            term = pair_term(a, b)
-                            found = term if found is None else found + term
-                        news.append(found)
-                    for row_id, old, new in zip(ids, olds, news):
-                        total[row_id] = old + new
-                    while len(news) > 1:
-                        news = [m + n for m, n in zip(news[0::2], news[1::2])]
-                    return own + news[0]
-
-                own = lax.fori_loop(
-                    0, table[first, STEPS_PLACE], of_rows, jnp.zeros((8, LANES), jnp.float32)
-                )
-                total[first * GROUPS] = total[first * GROUPS] + own
-
-        return carry
-
-    lax.fori_loop(0, ROBOTS, of_robot, 0)
-
-    for robot in range(ROBOTS):
-        found = total[robot * GROUPS]
-        for group in range(1, GROUPS):
-            found = found + total[robot * GROUPS + group]
-        turned[robot, 0] = found
-    cost = jnp.sum(turned[:, 0], axis=1)
-    for shift in (64, 32, 16):
-        cost = cost + pltpu.roll(cost, shift, 1)
-    cost = cost * (1.0 / (SPHERES * SPHERES))
-    for device in range(ROBOT_DEVICES):
-        cost_ref[device] = cost[ROBOTS_HERE * device : ROBOTS_HERE * (device + 1), :]
+    lax.fori_loop(0, (ROW_IDS + 1) // 15, clear, 0)
+
+    def row_ids(words):
+        return [lax.shift_right_logical(word, 8 * n) & 255 for word in words for n in range(4)]
+
+    def sum_terms(groups, n):
+        terms = [jnp.exp2(arguments[n * groups + group]) for group in range(groups)]
+        while len(terms) > 1:
+            terms = [p + q for p, q in zip(terms[0::2], terms[1::2])] + terms[len(terms) & ~1 :]
+        return terms[0]
+
+    def add_up(ids, news):
+        own = news
+        while len(own) > 1:
+            own = [p + q for p, q in zip(own[0::2], own[1::2])]
+        olds = [total[row_id] for row_id in ids]
+        for row_id, old, new in zip(ids, olds, news + own):
+            total[row_id] = old + new
+
+    def entry_of(turn, step):
+        robot = jnp.minimum(table[ORDER + turn], ROBOTS - 1)
+        at = robot * ENTRY + 2 * step
+        return robot, table[at], table[at + 1]
+
+    for groups in range(FIRST_GROUPS, GROUPS + 1):
+
+        def one_step(_, state, groups=groups):
+            turn, step, robot, first, second, *past_ids = state
+            ids = row_ids((first, second)) + [robot * GROUPS]
+            a_row = robot * (4 * GROUPS)
+            news = []
+            for n in range(STEP_ROWS):
+                news.append(sum_terms(groups, n))
+                b = [
+                    jnp.broadcast_to(rows[pl.ds(ids[n] * 4 + q, 1), :], (8, LANES))
+                    for q in range(4)
+                ]
+                for group in range(groups):
+                    a = [turned[a_row + (group * 4 + q)] for q in range(4)]
+                    arguments[n * groups + group] = pair_argument(a, b)
+            add_up(past_ids, news)
+            step = step + 1
+            over = (step >= table[robot * ENTRY + STEPS_WORD]).astype(jnp.int32)
+            turn, step = turn + over, step * (1 - over)
+            return turn, step, *entry_of(turn, step), *ids
+
+        case = groups - FIRST_GROUPS
+        turn = table[CASE_START + case]
+        nothing = [jnp.int32(ROW_IDS)] * (STEP_ROWS + 1)
+        state = (turn, jnp.int32(0), *entry_of(turn, 0), *nothing)
+        state = lax.fori_loop(0, table[CASE_STEPS + case], one_step, state)
+        add_up(list(state[5:]), [sum_terms(groups, n) for n in range(STEP_ROWS)])
 
 
 def blend_kernel(
-    cost_ref,
+    total,
     self_ref,
     centres_ref,
     robot_cost_ref,
     gathered,
+    sums,
+    cost_ref,
     cost_recv,
     weight,
     packed,
@@ -305,6 +378,19 @@
     for peer in z_peers:
         pl.semaphore_signal(barrier, inc=1, device_id=(me, x * Z + peer), device_id_type=MESH)
     pl.semaphore_signal(barrier, inc=1, device_id=(me, opposite), device_id_type=MESH)
+
+    for robot in range(ROBOTS):
+        found = total[robot * GROUPS]
+        for group in range(1, GROUPS):
+            found = found + total[robot * GROUPS + group]
+        sums[robot] = found
+    cost = jnp.sum(sums[...], axis=1)
+    for shift in (64, 32, 16):
+        cost = cost + pltpu.roll(cost, shift, 1)
+    cost = cost * (1.0 / (SPHERES * SPHERES))
+    for device in range(ROBOT_DEVICES):
+        cost_ref[device] = cost[ROBOTS_HERE * device : ROBOTS_HERE * (device + 1), :]
+
     pl.semaphore_wait(barrier, ROBOT_DEVICES - 1 + Z)
 
     def start(src, dst, sems, number, device):
@@ -340,11 +426,11 @@
                 lane & bit != 0, pltpu.roll(cost, bit, 1), pltpu.roll(cost, LANES - bit, 1)
             )
         weight[half] = 1.0 / (1.0 + cost)
-    sums = weight[0] + weight[1]
-    sums = sums + pltpu.roll(sums, 64, 1)
-    sums = sums + pltpu.roll(sums, 32, 1)
+    weights = weight[0] + weight[1]
+    weights = weights + pltpu.roll(weights, 64, 1)
+    weights = weights + pltpu.roll(weights, 32, 1)
     line = iota(1, (1, LANES))
-    total_row = jnp.where(line < 64, sums[0:1, :], sums[1:2, :])
+    total_row = jnp.where(line < 64, weights[0:1, :], weights[1:2, :])
 
     quarter = iota(1) // W
     units = [[], []]
@@ -438,21 +524,28 @@
     peers = ROBOT_DEVICES - 1
     rows = centres.transpose(1, 2, 0, 3).reshape(3 * SPHERES, ROBOTS_HERE, 2, LANES)
     rows = rows.transpose(0, 2, 1, 3).reshape(3 * SPHERES * 2 * ROBOTS_HERE, LANES)
-    received, self_cost, table = pl.pallas_call(
+    in_hbm = pl.BlockSpec(memory_space=pltpu.HBM)
+    received, turned, self_cost, table = pl.pallas_call(
         spread_kernel,
         out_shape=(
             jax.ShapeDtypeStruct((ROBOT_DEVICES * ROWS + 8, LANES), f32),
+            jax.ShapeDtypeStruct((ROBOT_DEVICES * ROWS, 8, LANES), f32),
             jax.ShapeDtypeStruct((2 * ROBOTS_HERE, LANES), f32),
-            jax.ShapeDtypeStruct((ROBOTS, LIST + LANES), jnp.int32),
+            jax.ShapeDtypeStruct((TABLE_ROWS, LANES), jnp.int32),
         ),
-        in_specs=[IN_SMEM] + in_vmem(3),
-        out_specs=tuple(in_vmem(3)),
+        in_specs=[in_hbm] * 4,
+        out_specs=tuple(in_vmem(4)),
         scratch_shapes=[
+            pltpu.SMEM((ROBOTS_HERE,), jnp.int32),
+            pltpu.VMEM(rows.shape, f32),
+            pltpu.VMEM((ROBOTS_HERE, SPHERES), f32),
+            pltpu.VMEM((ROBOTS_HERE, ROBOTS), jnp.int32),
             pltpu.VMEM((ROBOT_DEVICES * ROWS, LANES), f32),
             pltpu.VMEM((2 * ROBOTS_HERE, 4, 64, LANES), f32),
             pltpu.VMEM((ROBOTS_HERE, LANES), jnp.int32),
             pltpu.VMEM((ROBOT_DEVICES, ROBOTS_HERE, LANES), jnp.int32),
             pltpu.VMEM((ROBOTS, LANES), jnp.int32),
+            dma((9,)),
             dma((peers,)),
             dma((peers,)),
             dma((peers,)),
@@ -462,19 +555,16 @@
             collective_id=0, has_side_effects=True, vmem_limit_bytes=GRANT
         ),
         name="spread",
-    )(counts, rows, sphere_radius, adjacency)
-    cost = pl.pallas_call(
+    )(*[pltpu.with_memory_space_constraint(v, pltpu.HBM) for v in (counts, rows, sphere_radius, adjacency)])
+    total = pl.pallas_call(
         cross_kernel,
-        out_shape=jax.ShapeDtypeStruct((ROBOT_DEVICES, ROBOTS_HERE, LANES), f32),
-        in_specs=[IN_SMEM] + in_vmem(1),
+        out_shape=jax.ShapeDtypeStruct((ROW_IDS + 1, 8, LANES), f32),
+        in_specs=[IN_SMEM] + in_vmem(2),
         out_specs=in_vmem(1)[0],
-        scratch_shapes=[
-            pltpu.VMEM((ROBOTS, 4 * GROUPS, 8, LANES), f32),
-            pltpu.VMEM((ROW_IDS + 1, 8, LANES), f32),
-        ],
+        scratch_shapes=[pltpu.VMEM((STEP_ROWS * GROUPS, 8, LANES), f32)],
         compiler_params=pltpu.CompilerParams(vmem_limit_bytes=GRANT),
         name="cross",
-    )(table, received)
+    )(table.reshape(TABLE_ROWS * LANES), received, turned)
     robot_cost, gathered = pl.pallas_call(
         blend_kernel,
         out_shape=(
@@ -484,6 +574,8 @@
         in_specs=in_vmem(3),
         out_specs=tuple(in_vmem(2)),
         scratch_shapes=[
+            pltpu.VMEM((ROBOTS, 8, LANES), f32),
+            pltpu.VMEM((ROBOT_DEVICES, ROBOTS_HERE, LANES), f32),
             pltpu.VMEM((ROBOT_DEVICES, ROBOTS_HERE, LANES), f32),
             pltpu.VMEM((2, ROBOTS_HERE, LANES), f32),
             pltpu.VMEM((Z, CHUNK + 1, LANES), f32),
@@ -499,7 +591,7 @@
             collective_id=1, has_side_effects=True, vmem_limit_bytes=GRANT
         ),
         name="blend",
-    )(cost, self_cost, rows)
+    )(total, self_cost, rows)
     robot_cost, blended = pl.pallas_call(
         finish_kernel,
         out_shape=(

time: 56.3 us -> 57.7 us (1.025)
  the two profiles are of different devices: /device:TPU:2 before, /device:TPU:8 now
where the time goes in v3:
time: 57.7 us; the launch traced here: 58.1 us
  Pallas kernels  57.4 us (99%)
  between operations  0.66 us (1%)
    pallas_call x1, Pallas kernels, local(): pl.pallas_call(blend_kernel, out_shape=(jax.ShapeDtypeStruct((ROBOTS_HERE...  28.5 us
    pallas_call x1, Pallas kernels, local(): pl.pallas_call(spread_kernel, out_shape=(jax.ShapeDtypeStruct((ROBOT_DEVI...  18.9 us
    pallas_call x1, Pallas kernels, local(): pl.pallas_call(cross_kernel, out_shape=jax.ShapeDtypeStruct((ROW_IDS + 1,...  9.19 us

profile of v3, /device:TPU:8, one launch (start us, length us, event | category | flops | bytes accessed | tf_op | source)
XLA Modules:
  0.0 58.1 jit_solution(11911948433666753105)
XLA Ops:
  0.6 0.0 copy-start
  0.6 18.9 %spread.1 = (f32[904,128]{1,0:T(8,128)S(1)}, f32[896,8,128]{2,1,0:T(8,128)S(1)}, f32[4,128]{1,0:T(4,128)S(1)}, s32[24,128]{1,0:T(8,128)S(1)}) custom-call(s32[2]{0:T(128)} %counts_hbm.1, f32[624,128]{1,0:T(8,128)} %bitcast.9, f32[2,52]{1,0:T(2,128)} %radius_hbm.1, s32[2,32]{1,0:T(2,128)} %adjacency_hbm.1), custom_call_target="tpu_custom_call" | custom-call | tf_op jit(solution)/shard_map/spread/pallas_call | solution.py:528
  19.6 9.2 %cross.1.total = f32[225,8,128]{2,1,0:T(8,128)S(1)} custom-call(s32[3072]{0:T(1024)S(1)} %bitcast.11, f32[904,128]{1,0:T(8,128)S(1)} %get-tuple-element.11.rows, f32[896,8,128]{2,1,0:T(8,128)S(1)} %get-tuple-element.12.turned), custom_call_target="tpu_custom_call" | custom-call | tf_op jit(solution)/shard_map/cross/pallas_call | solution.py:559
  28.8 0.0 copy-done
  28.8 28.5 %blend.1 = (f32[2,256]{1,0:T(2,128)S(1)}, f32[8,12,128]{2,1,0:T(8,128)S(1)}) custom-call(f32[225,8,128]{2,1,0:T(8,128)S(1)} %cross.1.total, f32[4,128]{1,0:T(4,128)S(1)} %get-tuple-element.13.self_ref, f32[624,128]{1,0:T(8,128)S(1)} %bitcast.10), custom_call_target="tpu_custom_call" | custom-call | tf_op jit(solution)/shard_map/blend/pallas_call | solution.py:568
  57.3 0.8 %finish.1 = (f32[2,256]{1,0:T(2,128)}, f32[2,3,32,52]{3,2,1,0:T(8,128)}) custom-call(f32[2,256]{1,0:T(2,128)S(1)} %get-tuple-element.14.cost_in, f32[8,12,128]{2,1,0:T(8,128)S(1)} %get-tuple-element.15.gathered), custom_call_target="tpu_custom_call" | custom-call | tf_op jit(solution)/shard_map/finish/pallas_call | solution.py:595
Async XLA Ops:
  0.6 28.1 %copy-start = (f32[2,3,52,256]{3,0,2,1:T(2,128)S(1)}, f32[2,3,52,256]{3,0,2,1:T(2,128)}, u32[]{:S(2)}) copy-start(f32[2,3,52,256]{3,0,2,1:T(2,128)} %param.4) | copy-start | bytes 958468

commit v4 on v3

--- a/solution.py
+++ b/solution.py
@@ -87,10 +87,6 @@
     seed = lax.axis_index("seed")
     peers = [lax.rem(me + step, ROBOT_DEVICES) for step in range(1, ROBOT_DEVICES)]
 
-    barrier = pltpu.get_barrier_semaphore()
-    for peer in peers:
-        pl.semaphore_signal(barrier, inc=1, device_id=(peer, seed), device_id_type=MESH)
-
     loads = [
         pltpu.make_async_copy(counts_hbm, counts_ref, load_sem.at[0]),
         pltpu.make_async_copy(radius_hbm, radius_ref, load_sem.at[1]),
@@ -105,6 +101,11 @@
         loads.append(pltpu.make_async_copy(centres_hbm.at[at], centres_ref.at[at], load_sem.at[6 + axis]))
     for load in loads:
         load.start()
+
+    barrier = pltpu.get_barrier_semaphore()
+    for peer in peers:
+        pl.semaphore_signal(barrier, inc=1, device_id=(peer, seed), device_id_type=MESH)
+
     for load in loads[:6]:
         load.wait()
 
@@ -160,19 +161,19 @@
     def rows_of(slot):
         return pl.ds(pl.multiple_of(slot * ROWS, 8), ROWS)
 
-    notes, copies = [], []
-    for number, peer in enumerate(peers):
-        copy = pltpu.make_async_remote_copy(
+    def send_note(number):
+        return pltpu.make_async_remote_copy(
             src_ref=note_send,
             dst_ref=note_recv.at[me],
             send_sem=note_send_sem.at[number],
             recv_sem=note_recv_sem.at[number],
-            device_id=(peer, seed),
+            device_id=(lax.rem(me + 1 + number, ROBOT_DEVICES), seed),
             device_id_type=MESH,
         )
-        copy.start()
-        notes.append(copy)
-        copy = pltpu.make_async_remote_copy(
+
+    def send_rows(number):
+        peer = lax.rem(me + 1 + number, ROBOT_DEVICES)
+        return pltpu.make_async_remote_copy(
             src_ref=send.at[rows_of(slot_of(peer))],
             dst_ref=recv_ref.at[rows_of(me)],
             send_sem=send_sem.at[number],
@@ -180,20 +181,24 @@
             device_id=(peer, seed),
             device_id_type=MESH,
         )
-        copy.start()
-        copies.append(copy)
+
+    def for_peers(act):
+        def one(number, carry):
+            act(number)
+            return carry
+
+        lax.fori_loop(0, ROBOT_DEVICES - 1, one, 0)
+
+    for_peers(lambda number: send_note(number).start())
+    for_peers(lambda number: send_rows(number).start())
     note_recv[me] = note_send[...]
     recv_ref[rows_of(me), :] = send[rows_of(slot_of(me)), :]
 
     def turn_rows(device):
-        def turn_group(index, carry):
-            row = pl.multiple_of(device * ROWS + index * 8, 8)
-            for n in range(8):
-                line = jnp.broadcast_to(recv_ref[pl.ds(row + n, 1), :], (8, LANES))
-                turned_ref[row + n] = pltpu.roll(line, 0, 1, stride=PART, stride_axis=0)
-            return carry
-
-        lax.fori_loop(0, ROWS // 8, turn_group, 0)
+        row = pl.multiple_of(device * ROWS, 8)
+        for n in range(ROWS):
+            line = jnp.broadcast_to(recv_ref[pl.ds(row + n, 1), :], (8, LANES))
+            turned_ref[row + n] = pltpu.roll(line, 0, 1, stride=PART, stride_axis=0)
 
     turn_rows(me)
     for index in range(2 * ROBOTS_HERE):
@@ -221,8 +226,7 @@
 
     lax.fori_loop(0, 2 * ROBOTS_HERE, self_pairs, 0)
 
-    for copy in notes:
-        copy.wait_recv()
+    for_peers(lambda number: send_note(number).wait_recv())
     for device in range(ROBOT_DEVICES):
         note[ROBOTS_HERE * device : ROBOTS_HERE * (device + 1), :] = note_recv[device]
     shape = (ROBOTS, LANES)
@@ -275,11 +279,13 @@
         sub == 0, -1000.0 * FAR, jnp.where(sub == 3, 1.0, 0.0)
     )
 
-    for number, copy in enumerate(copies):
-        copy.wait_recv()
+    def arrive(number):
+        send_rows(number).wait_recv()
         turn_rows(lax.rem(me + ROBOT_DEVICES - 1 - number, ROBOT_DEVICES))
-    for copy in notes + copies:
-        copy.wait_send()
+
+    for_peers(arrive)
+    for_peers(lambda number: send_note(number).wait_send())
+    for_peers(lambda number: send_rows(number).wait_send())
 
 
 def cross_kernel(table, rows, turned, total, arguments):

time: 57.7 us -> 49.9 us (0.86)
  the two profiles are of different devices: /device:TPU:8 before, /device:TPU:2 now
where the time goes in v4:
time: 49.9 us; the launch traced here: 49.7 us
  Pallas kernels  49 us (98%)
  between operations  0.66 us (1%)
    pallas_call x1, Pallas kernels, local(): pl.pallas_call(blend_kernel, out_shape=(jax.ShapeDtypeStruct((ROBOTS_HERE...  26.5 us
    pallas_call x1, Pallas kernels, local(): pl.pallas_call(spread_kernel, out_shape=(jax.ShapeDtypeStruct((ROBOT_DEVI...  13 us
    pallas_call x1, Pallas kernels, local(): pl.pallas_call(cross_kernel, out_shape=jax.ShapeDtypeStruct((ROW_IDS + 1,...  8.69 us

profile of v4, /device:TPU:2, one launch (start us, length us, event | category | flops | bytes accessed | tf_op | source)
XLA Modules:
  0.0 49.7 jit_solution(927792705086446765)
XLA Ops:
  0.6 0.0 copy-start
  0.6 13.0 %spread.1 = (f32[904,128]{1,0:T(8,128)S(1)}, f32[896,8,128]{2,1,0:T(8,128)S(1)}, f32[4,128]{1,0:T(4,128)S(1)}, s32[24,128]{1,0:T(8,128)S(1)}) custom-call(s32[2]{0:T(128)} %counts_hbm.1, f32[624,128]{1,0:T(8,128)} %bitcast.9, f32[2,52]{1,0:T(2,128)} %radius_hbm.1, s32[2,32]{1,0:T(2,128)} %adjacency_hbm.1), custom_call_target="tpu_custom_call" | custom-call | tf_op jit(solution)/shard_map/spread/pallas_call | solution.py:534
  13.7 8.7 %cross.1.total = f32[225,8,128]{2,1,0:T(8,128)S(1)} custom-call(s32[3072]{0:T(1024)S(1)} %bitcast.11, f32[904,128]{1,0:T(8,128)S(1)} %get-tuple-element.11.rows, f32[896,8,128]{2,1,0:T(8,128)S(1)} %get-tuple-element.12.turned), custom_call_target="tpu_custom_call" | custom-call | tf_op jit(solution)/shard_map/cross/pallas_call | solution.py:565
  22.4 0.0 copy-done
  22.4 26.5 %blend.1 = (f32[2,256]{1,0:T(2,128)S(1)}, f32[8,12,128]{2,1,0:T(8,128)S(1)}) custom-call(f32[225,8,128]{2,1,0:T(8,128)S(1)} %cross.1.total, f32[4,128]{1,0:T(4,128)S(1)} %get-tuple-element.13.self_ref, f32[624,128]{1,0:T(8,128)S(1)} %bitcast.10), custom_call_target="tpu_custom_call" | custom-call | tf_op jit(solution)/shard_map/blend/pallas_call | solution.py:574
  48.9 0.8 %finish.1 = (f32[2,256]{1,0:T(2,128)}, f32[2,3,32,52]{3,2,1,0:T(8,128)}) custom-call(f32[2,256]{1,0:T(2,128)S(1)} %get-tuple-element.14.cost_in, f32[8,12,128]{2,1,0:T(8,128)S(1)} %get-tuple-element.15.gathered), custom_call_target="tpu_custom_call" | custom-call | tf_op jit(solution)/shard_map/finish/pallas_call | solution.py:601
Async XLA Ops:
  0.6 21.7 %copy-start = (f32[2,3,52,256]{3,0,2,1:T(2,128)S(1)}, f32[2,3,52,256]{3,0,2,1:T(2,128)}, u32[]{:S(2)}) copy-start(f32[2,3,52,256]{3,0,2,1:T(2,128)} %param.4) | copy-start | bytes 958468

commit v5 on v4

--- a/solution.py
+++ b/solution.py
@@ -288,10 +288,8 @@
     for_peers(lambda number: send_rows(number).wait_send())
 
 
-def cross_kernel(table, rows, turned, total, arguments):
+def cross_kernel(table, rows, turned, total):
     zero = jnp.zeros((8, LANES), jnp.float32)
-    for slot in range(STEP_ROWS * GROUPS):
-        arguments[slot] = zero
 
     def clear(index, carry):
         for n in range(15):
@@ -300,56 +298,63 @@
 
     lax.fori_loop(0, (ROW_IDS + 1) // 15, clear, 0)
 
-    def row_ids(words):
-        return [lax.shift_right_logical(word, 8 * n) & 255 for word in words for n in range(4)]
-
-    def sum_terms(groups, n):
-        terms = [jnp.exp2(arguments[n * groups + group]) for group in range(groups)]
-        while len(terms) > 1:
-            terms = [p + q for p, q in zip(terms[0::2], terms[1::2])] + terms[len(terms) & ~1 :]
-        return terms[0]
-
-    def add_up(ids, news):
-        own = news
+    def pair_sums(groups, robot, ids):
+        a_row = robot * (4 * GROUPS)
+        sums = []
+        for row_id in ids:
+            b = [
+                jnp.broadcast_to(rows[pl.ds(row_id * 4 + q, 1), :], (8, LANES)) for q in range(4)
+            ]
+            terms = []
+            for group in range(groups):
+                a = [turned[a_row + (group * 4 + q)] for q in range(4)]
+                terms.append(pair_term(a, b))
+            while len(terms) > 1:
+                terms = [p + q for p, q in zip(terms[0::2], terms[1::2])] + terms[len(terms) & ~1 :]
+            sums.append(terms[0])
+        return sums
+
+    def add_up(robot, ids, found):
+        own = found
         while len(own) > 1:
             own = [p + q for p, q in zip(own[0::2], own[1::2])]
+        ids = ids + [robot * GROUPS]
         olds = [total[row_id] for row_id in ids]
-        for row_id, old, new in zip(ids, olds, news + own):
+        for row_id, old, new in zip(ids, olds, found + own):
             total[row_id] = old + new
 
-    def entry_of(turn, step):
+    nothing = ROW_IDS * 0x01010101 - (1 << 32)
+
+    def step_of(turn, step, there):
         robot = jnp.minimum(table[ORDER + turn], ROBOTS - 1)
-        at = robot * ENTRY + 2 * step
-        return robot, table[at], table[at + 1]
+        entry = robot * ENTRY
+        words = [
+            jnp.where(there, table[entry + 2 * step + n], jnp.int32(nothing)) for n in range(2)
+        ]
+        ids = [lax.shift_right_logical(word, 8 * n) & 255 for word in words for n in range(4)]
+        step = step + 1
+        over = (step >= table[entry + STEPS_WORD]).astype(jnp.int32)
+        return robot, ids, jnp.minimum(turn + over, ROBOTS - 1), step * (1 - over)
 
     for groups in range(FIRST_GROUPS, GROUPS + 1):
-
-        def one_step(_, state, groups=groups):
-            turn, step, robot, first, second, *past_ids = state
-            ids = row_ids((first, second)) + [robot * GROUPS]
-            a_row = robot * (4 * GROUPS)
-            news = []
-            for n in range(STEP_ROWS):
-                news.append(sum_terms(groups, n))
-                b = [
-                    jnp.broadcast_to(rows[pl.ds(ids[n] * 4 + q, 1), :], (8, LANES))
-                    for q in range(4)
-                ]
-                for group in range(groups):
-                    a = [turned[a_row + (group * 4 + q)] for q in range(4)]
-                    arguments[n * groups + group] = pair_argument(a, b)
-            add_up(past_ids, news)
-            step = step + 1
-            over = (step >= table[robot * ENTRY + STEPS_WORD]).astype(jnp.int32)
-            turn, step = turn + over, step * (1 - over)
-            return turn, step, *entry_of(turn, step), *ids
-
-        case = groups - FIRST_GROUPS
-        turn = table[CASE_START + case]
-        nothing = [jnp.int32(ROW_IDS)] * (STEP_ROWS + 1)
-        state = (turn, jnp.int32(0), *entry_of(turn, 0), *nothing)
-        state = lax.fori_loop(0, table[CASE_STEPS + case], one_step, state)
-        add_up(list(state[5:]), [sum_terms(groups, n) for n in range(STEP_ROWS)])
+        steps = table[CASE_STEPS + groups - FIRST_GROUPS]
+
+        def two_steps_of(index, turn, step):
+            robot, ids, turn, step = step_of(turn, step, 2 * index < steps)
+            other, other_ids, turn, step = step_of(turn, step, 2 * index + 1 < steps)
+            return turn, step, robot, other, *ids, *other_ids
+
+        def two_steps(index, state, groups=groups, two_steps_of=two_steps_of):
+            turn, step, robot, other, *ids = state
+            ids, other_ids = ids[:STEP_ROWS], ids[STEP_ROWS:]
+            found = pair_sums(groups, robot, ids)
+            other_found = pair_sums(groups, other, other_ids)
+            add_up(robot, ids, found)
+            add_up(other, other_ids, other_found)
+            return two_steps_of(index + 1, turn, step)
+
+        start = jnp.minimum(table[CASE_START + groups - FIRST_GROUPS], ROBOTS - 1)
+        lax.fori_loop(0, (steps + 1) >> 1, two_steps, two_steps_of(0, start, jnp.int32(0)))
 
 
 def blend_kernel(
@@ -364,26 +369,23 @@
     weight,
     packed,
     parts,
-    mine,
-    other,
     cost_sems,
     part_sems,
-    pair_sems,
     gather_sems,
 ):
     me = lax.axis_index("robot")
     seed = lax.axis_index("seed")
     x, z = seed // Z, lax.rem(seed, Z)
     peers = [lax.rem(me + step, ROBOT_DEVICES) for step in range(1, ROBOT_DEVICES)]
-    z_peers = [lax.rem(z + step, Z) for step in range(1, Z)]
-    opposite = (1 - x) * Z + z
+    z_peers = [lax.rem(z + step, Z) for step in (4, 3, 5, 2, 6, 1, 7)]
+    seed_peers = [lax.rem((1 - x) * Z + lax.rem(z + 4, Z), 2 * Z)] + [p for step in (3, 5, 2, 6, 1, 7, 0) for p in ([(1 - x) * Z + lax.rem(z + step, Z)])]
+    seed_peers = seed_peers[:3] + [x * Z + lax.rem(z + 4, Z)] + seed_peers[3:5] + [x * Z + lax.rem(z + 3, Z), x * Z + lax.rem(z + 5, Z)] + seed_peers[5:7] + [x * Z + lax.rem(z + 2, Z), x * Z + lax.rem(z + 6, Z)] + seed_peers[7:] + [x * Z + lax.rem(z + 1, Z), x * Z + lax.rem(z + 7, Z)]
 
     barrier = pltpu.get_barrier_semaphore()
     for peer in peers:
         pl.semaphore_signal(barrier, inc=1, device_id=(peer, seed), device_id_type=MESH)
-    for peer in z_peers:
-        pl.semaphore_signal(barrier, inc=1, device_id=(me, x * Z + peer), device_id_type=MESH)
-    pl.semaphore_signal(barrier, inc=1, device_id=(me, opposite), device_id_type=MESH)
+    for peer in seed_peers:
+        pl.semaphore_signal(barrier, inc=1, device_id=(me, peer), device_id_type=MESH)
 
     for robot in range(ROBOTS):
         found = total[robot * GROUPS]
@@ -397,7 +399,7 @@
     for device in range(ROBOT_DEVICES):
         cost_ref[device] = cost[ROBOTS_HERE * device : ROBOTS_HERE * (device + 1), :]
 
-    pl.semaphore_wait(barrier, ROBOT_DEVICES - 1 + Z)
+    pl.semaphore_wait(barrier, ROBOT_DEVICES - 1 + 2 * Z - 1)
 
     def start(src, dst, sems, number, device):
         copy = pltpu.make_async_remote_copy(
@@ -478,16 +480,10 @@
         found = found + parts[number]
     sent = sent + copies
 
-    mine[...] = found
-    copy = start(mine, other, pair_sems, 0, (me, opposite))
-    copy.wait_recv()
-    sent = sent + [copy]
-    found = mine[...] + other[...]
-    gathered[z] = found / found[CHUNK : CHUNK + 1, :]
-
+    gathered[seed] = found
     copies = [
-        start(gathered.at[z], gathered.at[z], gather_sems, number, (me, x * Z + peer))
-        for number, peer in enumerate(z_peers)
+        start(gathered.at[seed], gathered.at[seed], gather_sems, number, (me, peer))
+        for number, peer in enumerate(seed_peers)
     ]
     for copy in copies:
         copy.wait_recv()
@@ -500,7 +496,9 @@
 def finish_kernel(cost_in, gathered, cost_out, blended, lines):
     cost_out[...] = cost_in[...]
     for chunk in range(Z):
-        lines[CHUNK * chunk : CHUNK * (chunk + 1), :] = gathered[chunk, 0:CHUNK, :]
+        found = gathered[chunk] + gathered[Z + chunk]
+        found = found / found[CHUNK : CHUNK + 1, :]
+        lines[CHUNK * chunk : CHUNK * (chunk + 1), :] = found[0:CHUNK, :]
     turned = lines[...].T
     for robot in range(ROBOTS_HERE):
         for axis in range(3):
@@ -567,7 +565,6 @@
         out_shape=jax.ShapeDtypeStruct((ROW_IDS + 1, 8, LANES), f32),
         in_specs=[IN_SMEM] + in_vmem(2),
         out_specs=in_vmem(1)[0],
-        scratch_shapes=[pltpu.VMEM((STEP_ROWS * GROUPS, 8, LANES), f32)],
         compiler_params=pltpu.CompilerParams(vmem_limit_bytes=GRANT),
         name="cross",
     )(table.reshape(TABLE_ROWS * LANES), received, turned)
@@ -575,7 +572,7 @@
         blend_kernel,
         out_shape=(
             jax.ShapeDtypeStruct((ROBOTS_HERE, COLUMNS), f32),
-            jax.ShapeDtypeStruct((Z, CHUNK + 1, LANES), f32),
+            jax.ShapeDtypeStruct((2 * Z, CHUNK + 1, LANES), f32),
         ),
         in_specs=in_vmem(3),
         out_specs=tuple(in_vmem(2)),
@@ -586,12 +583,9 @@
             pltpu.VMEM((2, ROBOTS_HERE, LANES), f32),
             pltpu.VMEM((Z, CHUNK + 1, LANES), f32),
             pltpu.VMEM((Z - 1, CHUNK + 1, LANES), f32),
-            pltpu.VMEM((CHUNK + 1, LANES), f32),
-            pltpu.VMEM((CHUNK + 1, LANES), f32),
             dma((2, peers)),
             dma((2, Z - 1)),
-            dma((2, 1)),
-            dma((2, Z - 1)),
+            dma((2, 2 * Z - 1)),
         ],
         compiler_params=pltpu.CompilerParams(
             collective_id=1, has_side_effects=True, vmem_limit_bytes=GRANT

time: 49.9 us -> 48.1 us (0.964)
  the two profiles are of different devices: /device:TPU:2 before, /device:TPU:6 now
where the time goes in v5:
time: 48.1 us; the launch traced here: 47.6 us
  Pallas kernels  46.9 us (98%)
  between operations  0.67 us (1%)
    pallas_call x1, Pallas kernels, local(): pl.pallas_call(blend_kernel, out_shape=(jax.ShapeDtypeStruct((ROBOTS_HERE...  25.8 us
    pallas_call x1, Pallas kernels, local(): pl.pallas_call(spread_kernel, out_shape=(jax.ShapeDtypeStruct((ROBOT_DEVI...  12.4 us
    pallas_call x1, Pallas kernels, local(): pl.pallas_call(cross_kernel, out_shape=jax.ShapeDtypeStruct((ROW_IDS + 1,...  7.86 us

profile of v5, /device:TPU:6, one launch (start us, length us, event | category | flops | bytes accessed | tf_op | source)
XLA Modules:
  0.0 47.6 jit_solution(2598467357686644334)
XLA Ops:
  0.6 0.0 copy-start
  0.6 12.4 %spread.1 = (f32[904,128]{1,0:T(8,128)S(1)}, f32[896,8,128]{2,1,0:T(8,128)S(1)}, f32[4,128]{1,0:T(4,128)S(1)}, s32[24,128]{1,0:T(8,128)S(1)}) custom-call(s32[2]{0:T(128)} %counts_hbm.1, f32[624,128]{1,0:T(8,128)} %bitcast.9, f32[2,52]{1,0:T(2,128)} %radius_hbm.1, s32[2,32]{1,0:T(2,128)} %adjacency_hbm.1), custom_call_target="tpu_custom_call" | custom-call | tf_op jit(solution)/shard_map/spread/pallas_call | solution.py:532
  13.1 7.9 %cross.1.total = f32[225,8,128]{2,1,0:T(8,128)S(1)} custom-call(s32[3072]{0:T(1024)S(1)} %bitcast.11, f32[904,128]{1,0:T(8,128)S(1)} %get-tuple-element.11.rows, f32[896,8,128]{2,1,0:T(8,128)S(1)} %get-tuple-element.12.turned), custom_call_target="tpu_custom_call" | custom-call | tf_op jit(solution)/shard_map/cross/pallas_call | solution.py:563
  20.9 0.0 copy-done
  21.0 25.8 %blend.1 = (f32[2,256]{1,0:T(2,128)S(1)}, f32[16,12,128]{2,1,0:T(8,128)S(1)}) custom-call(f32[225,8,128]{2,1,0:T(8,128)S(1)} %cross.1.total, f32[4,128]{1,0:T(4,128)S(1)} %get-tuple-element.13.self_ref, f32[624,128]{1,0:T(8,128)S(1)} %bitcast.10), custom_call_target="tpu_custom_call" | custom-call | tf_op jit(solution)/shard_map/blend/pallas_call | solution.py:571
  46.8 0.8 %finish.1 = (f32[2,256]{1,0:T(2,128)}, f32[2,3,32,52]{3,2,1,0:T(8,128)}) custom-call(f32[2,256]{1,0:T(2,128)S(1)} %get-tuple-element.14.cost_in, f32[16,12,128]{2,1,0:T(8,128)S(1)} %get-tuple-element.15.gathered), custom_call_target="tpu_custom_call" | custom-call | tf_op jit(solution)/shard_map/finish/pallas_call | solution.py:595
Async XLA Ops:
  0.6 20.3 %copy-start = (f32[2,3,52,256]{3,0,2,1:T(2,128)S(1)}, f32[2,3,52,256]{3,0,2,1:T(2,128)}, u32[]{:S(2)}) copy-start(f32[2,3,52,256]{3,0,2,1:T(2,128)} %param.4) | copy-start | bytes 958468

commit v6 on v5

--- a/solution.py
+++ b/solution.py
@@ -32,6 +32,9 @@
 ORDER = ROBOTS * ENTRY
 CASE_STEPS = ORDER + 32
 CASE_START = ORDER + 40
+LATE = ORDER + 48
+LATE_STEPS = 12
+LATE_SLOTS = 112
 TABLE_ROWS = 24
 EARLY_GROUPS = 3
 GRANT = 16 * 1024 * 1024
@@ -268,12 +271,28 @@
     last = jnp.sum(
         jnp.where((rank == lane_number) & (busy > 0.0), row_number, 0.0), axis=0, keepdims=True
     )
+    steps_row = as_row(steps)
+    rank_row = as_row(rank)
+    done_before = jnp.sum(
+        jnp.where((rank_row < rank) & (busy_row > 0.0), steps_row, 0.0), axis=1, keepdims=True
+    )
+    all_steps = jnp.sum(steps_row, axis=1, keepdims=True)
+    late_start = jnp.maximum(all_steps - float(LATE_STEPS), 0.0)
+    holds = (busy > 0.0) & (done_before <= late_start) & (late_start < done_before + steps)
+
+    def held(value):
+        return jnp.sum(jnp.where(holds, value, 0.0), axis=0, keepdims=True)
+
     line = iota(1, (1, LANES))
+    for n, value in enumerate((held(rank), held(late_start - done_before), all_steps - late_start)):
+        last = jnp.where(line == LATE - ORDER + n, value, last)
     for case in range(FIRST_GROUPS, GROUPS + 1):
-        of_case = jnp.where(row == column, jnp.where(groups == float(case), steps, 0.0), 0.0)
-        earlier = jnp.where(row == column, jnp.where(groups < float(case), busy, 0.0), 0.0)
-        last = jnp.where(line == CASE_STEPS - ORDER + case - FIRST_GROUPS, jnp.sum(of_case), last)
-        last = jnp.where(line == CASE_START - ORDER + case - FIRST_GROUPS, jnp.sum(earlier), last)
+        of_case = jnp.sum(jnp.where(groups == float(case), steps, 0.0), axis=0, keepdims=True)
+        before_case = jnp.sum(jnp.where(groups < float(case), steps, 0.0), axis=0, keepdims=True)
+        earlier = jnp.sum(jnp.where(groups < float(case), busy, 0.0), axis=0, keepdims=True)
+        of_case = jnp.minimum(jnp.maximum(late_start - before_case, 0.0), of_case)
+        last = jnp.where(line == CASE_STEPS - ORDER + case - FIRST_GROUPS, of_case, last)
+        last = jnp.where(line == CASE_START - ORDER + case - FIRST_GROUPS, earlier, last)
     table_ref[16:24, :] = jnp.broadcast_to(last, (8, LANES)).astype(jnp.int32)
     recv_ref[ROBOT_DEVICES * ROWS : ROBOT_DEVICES * ROWS + 8, :] = jnp.where(
         sub == 0, -1000.0 * FAR, jnp.where(sub == 3, 1.0, 0.0)
@@ -288,6 +307,35 @@
     for_peers(lambda number: send_rows(number).wait_send())
 
 
+def pair_sums(rows, turned, groups, robot, ids):
+    a_row = robot * (4 * GROUPS)
+    sums = []
+    for row_id in ids:
+        b = [jnp.broadcast_to(rows[pl.ds(row_id * 4 + q, 1), :], (8, LANES)) for q in range(4)]
+        terms = []
+        for group in range(groups):
+            a = [turned[a_row + (group * 4 + q)] for q in range(4)]
+            terms.append(pair_term(a, b))
+        while len(terms) > 1:
+            terms = [p + q for p, q in zip(terms[0::2], terms[1::2])] + terms[len(terms) & ~1 :]
+        sums.append(terms[0])
+    own = sums
+    while len(own) > 1:
+        own = [p + q for p, q in zip(own[0::2], own[1::2])]
+    return sums + own
+
+
+def step_of(table, turn, step, there):
+    robot = jnp.minimum(table[ORDER + turn], ROBOTS - 1)
+    entry = robot * ENTRY
+    nothing = jnp.int32(ROW_IDS * 0x01010101 - (1 << 32))
+    words = [jnp.where(there, table[entry + 2 * step + n], nothing) for n in range(2)]
+    ids = [lax.shift_right_logical(word, 8 * n) & 255 for word in words for n in range(4)]
+    step = step + 1
+    over = (step >= table[entry + STEPS_WORD]).astype(jnp.int32)
+    return robot, ids, jnp.minimum(turn + over, ROBOTS - 1), step * (1 - over)
+
+
 def cross_kernel(table, rows, turned, total):
     zero = jnp.zeros((8, LANES), jnp.float32)
 
@@ -298,57 +346,25 @@
 
     lax.fori_loop(0, (ROW_IDS + 1) // 15, clear, 0)
 
-    def pair_sums(groups, robot, ids):
-        a_row = robot * (4 * GROUPS)
-        sums = []
-        for row_id in ids:
-            b = [
-                jnp.broadcast_to(rows[pl.ds(row_id * 4 + q, 1), :], (8, LANES)) for q in range(4)
-            ]
-            terms = []
-            for group in range(groups):
-                a = [turned[a_row + (group * 4 + q)] for q in range(4)]
-                terms.append(pair_term(a, b))
-            while len(terms) > 1:
-                terms = [p + q for p, q in zip(terms[0::2], terms[1::2])] + terms[len(terms) & ~1 :]
-            sums.append(terms[0])
-        return sums
-
     def add_up(robot, ids, found):
-        own = found
-        while len(own) > 1:
-            own = [p + q for p, q in zip(own[0::2], own[1::2])]
         ids = ids + [robot * GROUPS]
         olds = [total[row_id] for row_id in ids]
-        for row_id, old, new in zip(ids, olds, found + own):
+        for row_id, old, new in zip(ids, olds, found):
             total[row_id] = old + new
-
-    nothing = ROW_IDS * 0x01010101 - (1 << 32)
-
-    def step_of(turn, step, there):
-        robot = jnp.minimum(table[ORDER + turn], ROBOTS - 1)
-        entry = robot * ENTRY
-        words = [
-            jnp.where(there, table[entry + 2 * step + n], jnp.int32(nothing)) for n in range(2)
-        ]
-        ids = [lax.shift_right_logical(word, 8 * n) & 255 for word in words for n in range(4)]
-        step = step + 1
-        over = (step >= table[entry + STEPS_WORD]).astype(jnp.int32)
-        return robot, ids, jnp.minimum(turn + over, ROBOTS - 1), step * (1 - over)
 
     for groups in range(FIRST_GROUPS, GROUPS + 1):
         steps = table[CASE_STEPS + groups - FIRST_GROUPS]
 
         def two_steps_of(index, turn, step):
-            robot, ids, turn, step = step_of(turn, step, 2 * index < steps)
-            other, other_ids, turn, step = step_of(turn, step, 2 * index + 1 < steps)
+            robot, ids, turn, step = step_of(table, turn, step, 2 * index < steps)
+            other, other_ids, turn, step = step_of(table, turn, step, 2 * index + 1 < steps)
             return turn, step, robot, other, *ids, *other_ids
 
         def two_steps(index, state, groups=groups, two_steps_of=two_steps_of):
             turn, step, robot, other, *ids = state
             ids, other_ids = ids[:STEP_ROWS], ids[STEP_ROWS:]
-            found = pair_sums(groups, robot, ids)
-            other_found = pair_sums(groups, other, other_ids)
+            found = pair_sums(rows, turned, groups, robot, ids)
+            other_found = pair_sums(rows, turned, groups, other, other_ids)
             add_up(robot, ids, found)
             add_up(other, other_ids, other_found)
             return two_steps_of(index + 1, turn, step)
@@ -358,17 +374,24 @@
 
 
 def blend_kernel(
+    table_ref,
+    rows,
+    turned,
     total,
     self_ref,
     centres_ref,
     robot_cost_ref,
     gathered,
+    table,
+    late,
+    late_robot,
     sums,
     cost_ref,
     cost_recv,
     weight,
     packed,
     parts,
+    table_sem,
     cost_sems,
     part_sems,
     gather_sems,
@@ -387,12 +410,42 @@
     for peer in seed_peers:
         pl.semaphore_signal(barrier, inc=1, device_id=(me, peer), device_id_type=MESH)
 
+    load = pltpu.make_async_copy(table_ref, table, table_sem)
+    load.start()
+    line = iota(1, (1, LANES))
     for robot in range(ROBOTS):
         found = total[robot * GROUPS]
         for group in range(1, GROUPS):
             found = found + total[robot * GROUPS + group]
         sums[robot] = found
-    cost = jnp.sum(sums[...], axis=1)
+    for slot in range(9 * LATE_STEPS, LATE_SLOTS):
+        late[slot] = jnp.zeros((8, LANES), jnp.float32)
+        late_robot[slot : slot + 1, :] = jnp.zeros((1, LANES), jnp.float32)
+    load.wait()
+    late_count = table[LATE + 2]
+
+    def two_steps(index, place):
+        turn, step = place
+        first = step_of(table, turn, step, 2 * index < late_count)
+        second = step_of(table, *first[2:], 2 * index + 1 < late_count)
+        slot = 2 * (STEP_ROWS + 1) * index
+        for robot, ids, _, _ in (first, second):
+            found = pair_sums(rows, turned, GROUPS, robot, ids)
+            for value, holder in zip(found, [row_id // GROUPS for row_id in ids] + [robot]):
+                late[slot] = value
+                late_robot[pl.ds(slot, 1), :] = jnp.where(line == holder, 1.0, 0.0)
+                slot = slot + 1
+        return second[2:]
+
+    lax.fori_loop(0, LATE_STEPS // 2, two_steps, (table[LATE], table[LATE + 1]))
+    late_cost = lax.dot_general(
+        late_robot[...],
+        jnp.sum(late[...], axis=1),
+        (((0,), (0,)), ((), ())),
+        precision=lax.Precision.HIGHEST,
+        preferred_element_type=jnp.float32,
+    )
+    cost = jnp.sum(sums[...], axis=1) + late_cost[0:ROBOTS, :]
     for shift in (64, 32, 16):
         cost = cost + pltpu.roll(cost, shift, 1)
     cost = cost * (1.0 / (SPHERES * SPHERES))
@@ -437,7 +490,6 @@
     weights = weight[0] + weight[1]
     weights = weights + pltpu.roll(weights, 64, 1)
     weights = weights + pltpu.roll(weights, 32, 1)
-    line = iota(1, (1, LANES))
     total_row = jnp.where(line < 64, weights[0:1, :], weights[1:2, :])
 
     quarter = iota(1) // W
@@ -560,6 +612,7 @@
         ),
         name="spread",
     )(*[pltpu.with_memory_space_constraint(v, pltpu.HBM) for v in (counts, rows, sphere_radius, adjacency)])
+    flat_table = table.reshape(TABLE_ROWS * LANES)
     total = pl.pallas_call(
         cross_kernel,
         out_shape=jax.ShapeDtypeStruct((ROW_IDS + 1, 8, LANES), f32),
@@ -567,22 +620,26 @@
         out_specs=in_vmem(1)[0],
         compiler_params=pltpu.CompilerParams(vmem_limit_bytes=GRANT),
         name="cross",
-    )(table.reshape(TABLE_ROWS * LANES), received, turned)
+    )(flat_table, received, turned)
     robot_cost, gathered = pl.pallas_call(
         blend_kernel,
         out_shape=(
             jax.ShapeDtypeStruct((ROBOTS_HERE, COLUMNS), f32),
             jax.ShapeDtypeStruct((2 * Z, CHUNK + 1, LANES), f32),
         ),
-        in_specs=in_vmem(3),
+        in_specs=in_vmem(6),
         out_specs=tuple(in_vmem(2)),
         scratch_shapes=[
+            pltpu.SMEM((TABLE_ROWS * LANES,), jnp.int32),
+            pltpu.VMEM((LATE_SLOTS, 8, LANES), f32),
+            pltpu.VMEM((LATE_SLOTS, LANES), f32),
             pltpu.VMEM((ROBOTS, 8, LANES), f32),
             pltpu.VMEM((ROBOT_DEVICES, ROBOTS_HERE, LANES), f32),
             pltpu.VMEM((ROBOT_DEVICES, ROBOTS_HERE, LANES), f32),
             pltpu.VMEM((2, ROBOTS_HERE, LANES), f32),
             pltpu.VMEM((Z, CHUNK + 1, LANES), f32),
             pltpu.VMEM((Z - 1, CHUNK + 1, LANES), f32),
+            dma,
             dma((2, peers)),
             dma((2, Z - 1)),
             dma((2, 2 * Z - 1)),
@@ -591,7 +648,7 @@
             collective_id=1, has_side_effects=True, vmem_limit_bytes=GRANT
         ),
         name="blend",
-    )(total, self_cost, rows)
+    )(flat_table, received, turned, total, self_cost, rows)
     robot_cost, blended = pl.pallas_call(
         finish_kernel,
         out_shape=(

time: 48.1 us -> 47 us (0.977)
  the two profiles are of different devices: /device:TPU:6 before, /device:TPU:2 now
where the time goes in v6:
time: 47 us; the launch traced here: 46.5 us
  Pallas kernels  45.8 us (97%)
  between operations  0.67 us (1%)
    pallas_call x1, Pallas kernels, local(): pl.pallas_call(blend_kernel, out_shape=(jax.ShapeDtypeStruct((ROBOTS_HERE...  24.5 us
    pallas_call x1, Pallas kernels, local(): pl.pallas_call(spread_kernel, out_shape=(jax.ShapeDtypeStruct((ROBOT_DEVI...  13 us
    pallas_call x1, Pallas kernels, local(): pl.pallas_call(cross_kernel, out_shape=jax.ShapeDtypeStruct((ROW_IDS + 1,...  7.43 us

profile of v6, /device:TPU:2, one launch (start us, length us, event | category | flops | bytes accessed | tf_op | source)
XLA Modules:
  0.0 46.5 jit_solution(12397301846492512555)
XLA Ops:
  0.6 0.0 copy-start
  0.6 13.0 %spread.1 = (f32[904,128]{1,0:T(8,128)S(1)}, f32[896,8,128]{2,1,0:T(8,128)S(1)}, f32[4,128]{1,0:T(4,128)S(1)}, s32[24,128]{1,0:T(8,128)S(1)}) custom-call(s32[2]{0:T(128)} %counts_hbm.1, f32[624,128]{1,0:T(8,128)} %bitcast.9, f32[2,52]{1,0:T(2,128)} %radius_hbm.1, s32[2,32]{1,0:T(2,128)} %adjacency_hbm.1), custom_call_target="tpu_custom_call" | custom-call | tf_op jit(solution)/shard_map/spread/pallas_call | solution.py:584
  13.7 7.4 %cross.1.total = f32[225,8,128]{2,1,0:T(8,128)S(1)} custom-call(s32[3072]{0:T(1024)S(1)} %bitcast.11, f32[904,128]{1,0:T(8,128)S(1)} %get-tuple-element.11.rows, f32[896,8,128]{2,1,0:T(8,128)S(1)} %get-tuple-element.12.turned), custom_call_target="tpu_custom_call" | custom-call | tf_op jit(solution)/shard_map/cross/pallas_call | solution.py:616
  21.1 0.0 copy-done
  21.1 24.5 %blend.1 = (f32[2,256]{1,0:T(2,128)S(1)}, f32[16,12,128]{2,1,0:T(8,128)S(1)}) custom-call(s32[3072]{0:T(1024)S(1)} %bitcast.12, f32[904,128]{1,0:T(8,128)S(1)} %get-tuple-element.11.rows, f32[896,8,128]{2,1,0:T(8,128)S(1)} %get-tuple-element.12.turned, f32[225,8,128]{2,1,0:T(8,128)S(1)} %cross.1.total, f32[4,128]{1,0:T(4,128)S(1)} %get-tuple-element.13.self_ref, ...), custom_call_target="tpu_custom_call" | custom-call | tf_op jit(solution)/shard_map/blend/pallas_call | solution.py:624
  45.6 0.8 %finish.1 = (f32[2,256]{1,0:T(2,128)}, f32[2,3,32,52]{3,2,1,0:T(8,128)}) custom-call(f32[2,256]{1,0:T(2,128)S(1)} %get-tuple-element.14.cost_in, f32[16,12,128]{2,1,0:T(8,128)S(1)} %get-tuple-element.15.gathered), custom_call_target="tpu_custom_call" | custom-call | tf_op jit(solution)/shard_map/finish/pallas_call | solution.py:652
Async XLA Ops:
  0.6 20.5 %copy-start = (f32[2,3,52,256]{3,0,2,1:T(2,128)S(1)}, f32[2,3,52,256]{3,0,2,1:T(2,128)}, u32[]{:S(2)}) copy-start(f32[2,3,52,256]{3,0,2,1:T(2,128)} %param.4) | copy-start | bytes 958468

commit v7 on v6

--- a/solution.py
+++ b/solution.py
@@ -33,8 +33,8 @@
 CASE_STEPS = ORDER + 32
 CASE_START = ORDER + 40
 LATE = ORDER + 48
-LATE_STEPS = 12
-LATE_SLOTS = 112
+LATE_STEPS = 24
+LATE_SLOTS = 216
 TABLE_ROWS = 24
 EARLY_GROUPS = 3
 GRANT = 16 * 1024 * 1024
@@ -405,10 +405,20 @@
     seed_peers = seed_peers[:3] + [x * Z + lax.rem(z + 4, Z)] + seed_peers[3:5] + [x * Z + lax.rem(z + 3, Z), x * Z + lax.rem(z + 5, Z)] + seed_peers[5:7] + [x * Z + lax.rem(z + 2, Z), x * Z + lax.rem(z + 6, Z)] + seed_peers[7:] + [x * Z + lax.rem(z + 1, Z), x * Z + lax.rem(z + 7, Z)]
 
     barrier = pltpu.get_barrier_semaphore()
-    for peer in peers:
+
+    def greet(number, carry):
+        peer = lax.rem(me + 1 + lax.rem(number + 7, ROBOT_DEVICES - 1), ROBOT_DEVICES)
         pl.semaphore_signal(barrier, inc=1, device_id=(peer, seed), device_id_type=MESH)
-    for peer in seed_peers:
+        return carry
+
+    lax.fori_loop(0, ROBOT_DEVICES - 1, greet, 0)
+
+    def greet_seed(number, carry):
+        peer = lax.rem(seed + 1 + number, 2 * Z)
         pl.semaphore_signal(barrier, inc=1, device_id=(me, peer), device_id_type=MESH)
+        return carry
+
+    lax.fori_loop(0, 2 * Z - 1, greet_seed, 0)
 
     load = pltpu.make_async_copy(table_ref, table, table_sem)
     load.start()

time: 47 us -> 45.8 us (0.974)
  Pallas kernels: 45.8 us -> 44.5 us
    pallas_call x1, Pallas kernels: 7.43 us -> 5.96 us  [local(): pl.pallas_call(cross_kernel, out_shape=jax.ShapeDtypeStruct((ROW_IDS + 1,...]
where the time goes in v7:
time: 45.8 us; the launch traced here: 45.2 us
  Pallas kernels  44.5 us (97%)
  between operations  0.67 us (1%)
    pallas_call x1, Pallas kernels, local(): pl.pallas_call(blend_kernel, out_shape=(jax.ShapeDtypeStruct((ROBOTS_HERE...  24.7 us
    pallas_call x1, Pallas kernels, local(): pl.pallas_call(spread_kernel, out_shape=(jax.ShapeDtypeStruct((ROBOT_DEVI...  13 us
    pallas_call x1, Pallas kernels, local(): pl.pallas_call(cross_kernel, out_shape=jax.ShapeDtypeStruct((ROW_IDS + 1,...  5.96 us

profile of v7, /device:TPU:2, one launch (start us, length us, event | category | flops | bytes accessed | tf_op | source)
XLA Modules:
  0.0 45.2 jit_solution(10766316970495000265)
XLA Ops:
  0.6 0.0 copy-start
  0.6 13.0 %spread.1 = (f32[904,128]{1,0:T(8,128)S(1)}, f32[896,8,128]{2,1,0:T(8,128)S(1)}, f32[4,128]{1,0:T(4,128)S(1)}, s32[24,128]{1,0:T(8,128)S(1)}) custom-call(s32[2]{0:T(128)} %counts_hbm.1, f32[624,128]{1,0:T(8,128)} %bitcast.9, f32[2,52]{1,0:T(2,128)} %radius_hbm.1, s32[2,32]{1,0:T(2,128)} %adjacency_hbm.1), custom_call_target="tpu_custom_call" | custom-call | tf_op jit(solution)/shard_map/spread/pallas_call | solution.py:594
  13.7 6.0 %cross.1.total = f32[225,8,128]{2,1,0:T(8,128)S(1)} custom-call(s32[3072]{0:T(1024)S(1)} %bitcast.11, f32[904,128]{1,0:T(8,128)S(1)} %get-tuple-element.11.rows, f32[896,8,128]{2,1,0:T(8,128)S(1)} %get-tuple-element.12.turned), custom_call_target="tpu_custom_call" | custom-call | tf_op jit(solution)/shard_map/cross/pallas_call | solution.py:626
  19.6 0.0 copy-done
  19.7 24.7 %blend.1 = (f32[2,256]{1,0:T(2,128)S(1)}, f32[16,12,128]{2,1,0:T(8,128)S(1)}) custom-call(s32[3072]{0:T(1024)S(1)} %bitcast.12, f32[904,128]{1,0:T(8,128)S(1)} %get-tuple-element.11.rows, f32[896,8,128]{2,1,0:T(8,128)S(1)} %get-tuple-element.12.turned, f32[225,8,128]{2,1,0:T(8,128)S(1)} %cross.1.total, f32[4,128]{1,0:T(4,128)S(1)} %get-tuple-element.13.self_ref, ...), custom_call_target="tpu_custom_call" | custom-call | tf_op jit(solution)/shard_map/blend/pallas_call | solution.py:634
  44.3 0.8 %finish.1 = (f32[2,256]{1,0:T(2,128)}, f32[2,3,32,52]{3,2,1,0:T(8,128)}) custom-call(f32[2,256]{1,0:T(2,128)S(1)} %get-tuple-element.14.cost_in, f32[16,12,128]{2,1,0:T(8,128)S(1)} %get-tuple-element.15.gathered), custom_call_target="tpu_custom_call" | custom-call | tf_op jit(solution)/shard_map/finish/pallas_call | solution.py:662
Async XLA Ops:
  0.6 19.0 %copy-start = (f32[2,3,52,256]{3,0,2,1:T(2,128)S(1)}, f32[2,3,52,256]{3,0,2,1:T(2,128)}, u32[]{:S(2)}) copy-start(f32[2,3,52,256]{3,0,2,1:T(2,128)} %param.4) | copy-start | bytes 958468

commit v8 on v7

--- a/solution.py
+++ b/solution.py
@@ -19,6 +19,10 @@
 COLUMNS = 256
 PART = 16
 ROWS = ROBOTS_HERE * GROUPS * 4
+AXIS_ROWS = 14
+SHARED, NEXT = 6, 7
+RADII = 3 * AXIS_ROWS
+MESSAGE = RADII + 2
 Z = 8
 CHUNK = 11
 COUNT_LANE = 32
@@ -76,6 +80,7 @@
     radius_ref,
     adjacency_ref,
     send,
+    recv,
     swept,
     note_send,
     note_recv,
@@ -114,55 +119,78 @@
 
     sub, lane = iota(0), iota(1)
     part = lane // PART
+    spot = lane % PART
     last_waypoint = lane % W == W - 1
     radius_lane = iota(1, (8, SPHERES))
     radius_sub = iota(0, (8, SPHERES))
+    numbers = [(me * ROBOTS_HERE + robot) * 64 + 1 for robot in range(ROBOTS_HERE)]
+
+    def ahead_of(here):
+        return jnp.where(last_waypoint, here, pltpu.roll(here, LANES - 1, 1))
+
+    def radius_column(robot, group):
+        row = jnp.broadcast_to(radius_ref[robot : robot + 1, :], (8, SPHERES))
+        return jnp.sum(jnp.where(radius_lane == radius_sub + 8 * group, row, 0.0), axis=1, keepdims=True)
+
+    def by_part(value):
+        value = pltpu.roll(value, 0, 1, stride=PART, stride_axis=0)
+        for bit in (1, 2, 4):
+            value = jnp.where(part & bit != 0, pltpu.roll(value, 8 - bit, 0), value)
+        return value
+
     note_send[...] = jnp.zeros((ROBOTS_HERE, LANES), jnp.int32)
     note_send[:, 0:ROBOTS] = adjacency_ref[...]
     for robot in range(ROBOTS_HERE):
         note_send[robot : robot + 1, COUNT_LANE : COUNT_LANE + 1] = jnp.full((1, 1), counts_ref[robot], jnp.int32)
-    for group in range(GROUPS):
-        if group == EARLY_GROUPS:
+    def raw(robot, axis, group, half):
+        here = centre_rows(centres_ref, robot, axis, group, half)
+        sphere = sub + 8 * group
+        far = FAR * (sphere + numbers[robot]).astype(jnp.float32) if axis == 0 else 0.0
+        return jnp.where(sphere < counts_ref[robot], here, far)
+
+    groups_of = [(0, g) for g in range(6)] + [None, None] + [(1, g) for g in range(6)]
+    next_columns = [[jnp.zeros((8, LANES), jnp.float32) for _ in range(3)] for _ in range(2)]
+    radii = jnp.zeros((8, LANES), jnp.float32)
+    for place in sorted((p for p in range(AXIS_ROWS) if p != NEXT), key=lambda p: p % 8):
+        if place == EARLY_GROUPS:
             for load in loads[6:]:
                 load.wait()
-        for robot in range(ROBOTS_HERE):
-            count = counts_ref[robot]
-            radius_row = jnp.broadcast_to(radius_ref[robot : robot + 1, :], (8, SPHERES))
-            number = (me * ROBOTS_HERE + robot) * 64 + 1
-            radius = jnp.sum(
-                jnp.where(radius_lane == radius_sub + 8 * group, radius_row, 0.0),
-                axis=1,
-                keepdims=True,
+        if place == SHARED:
+            column = jnp.where(
+                sub < 4,
+                radius_column(0, GROUPS - 1),
+                pltpu.roll(jnp.broadcast_to(radius_column(1, GROUPS - 1), (8, LANES)), 4, 0),
             )
-            sphere = sub + 8 * group
-            active = sphere < count
-            far = FAR * (sphere + number).astype(jnp.float32)
-            for half in range(2):
-                out, square = [], None
-                for axis in range(3):
-                    here = centre_rows(centres_ref, robot, axis, group, half)
-                    ahead = jnp.where(last_waypoint, here, pltpu.roll(here, LANES - 1, 1))
-                    step = ahead - here
-                    square = step * step if square is None else square + step * step
-                    middle = (here + ahead) * (0.5 * ROOT)
-                    out.append(jnp.where(active, middle, far if axis == 0 else 0.0))
-                out.append(jnp.where(active, radius + 0.5 * jnp.sqrt(square + 1e-6), 1.0))
-                for quantity in range(4):
-                    value = out[quantity]
-                    swept[half * ROBOTS_HERE + robot, quantity, 8 * group : 8 * group + 8, :] = value
-                    value = pltpu.roll(value, 0, 1, stride=PART, stride_axis=0)
-                    for bit in (1, 2, 4):
-                        value = jnp.where(part & bit != 0, pltpu.roll(value, 8 - bit, 0), value)
-                    row = (robot * GROUPS + group) * 4 + quantity
-                    send[pl.ds(half * 8 * ROWS + row, 8, stride=ROWS), :] = value
+        else:
+            column = radius_column(*groups_of[place])
+        radii = jnp.where(spot == PART - 1 - place, column, radii)
+        for half in range(2):
+            for axis in range(3):
+                if place == SHARED:
+                    value = jnp.where(
+                        sub < 4,
+                        raw(0, axis, GROUPS - 1, half),
+                        pltpu.roll(raw(1, axis, GROUPS - 1, half), 4, 0),
+                    )
+                else:
+                    robot, group = groups_of[place]
+                    value = raw(robot, axis, group, half)
+                send[half * 8 : half * 8 + 8, axis * AXIS_ROWS + place, :] = by_part(value)
+                value = pltpu.roll(ahead_of(value), (LANES - place) % LANES, 1)
+                next_columns[half][axis] = jnp.where(
+                    spot == PART - 1 - place, value, next_columns[half][axis]
+                )
+    radii = by_part(radii)
+    for half in range(2):
+        for axis in range(3):
+            send[half * 8 : half * 8 + 8, axis * AXIS_ROWS + NEXT, :] = by_part(next_columns[half][axis])
+        send[half * 8 : half * 8 + 8, RADII, :] = radii
+        send[half * 8 : half * 8 + 8, RADII + 1, :] = radii
 
     pl.semaphore_wait(barrier, ROBOT_DEVICES - 1)
 
     def slot_of(device):
         return (device // 8) * 8 + lax.rem(8 - lax.rem(device, 8), 8)
-
-    def rows_of(slot):
-        return pl.ds(pl.multiple_of(slot * ROWS, 8), ROWS)
 
     def send_note(number):
         return pltpu.make_async_remote_copy(
@@ -177,8 +205,8 @@
     def send_rows(number):
         peer = lax.rem(me + 1 + number, ROBOT_DEVICES)
         return pltpu.make_async_remote_copy(
-            src_ref=send.at[rows_of(slot_of(peer))],
-            dst_ref=recv_ref.at[rows_of(me)],
+            src_ref=send.at[slot_of(peer)],
+            dst_ref=recv.at[me],
             send_sem=send_sem.at[number],
             recv_sem=recv_sem.at[number],
             device_id=(peer, seed),
@@ -195,15 +223,67 @@
     for_peers(lambda number: send_note(number).start())
     for_peers(lambda number: send_rows(number).start())
     note_recv[me] = note_send[...]
-    recv_ref[rows_of(me), :] = send[rows_of(slot_of(me)), :]
-
-    def turn_rows(device):
-        row = pl.multiple_of(device * ROWS, 8)
+    recv[me] = send[slot_of(me)]
+    shared_first = ((part + (8 - lax.rem(me, 8))) & 7) < 4
+
+    def take(device):
+        base = device * ROWS
+        square = [None, None]
+        values = [[], []]
+        for axis in range(3):
+            following = jnp.broadcast_to(
+                recv[device, axis * AXIS_ROWS + NEXT : axis * AXIS_ROWS + NEXT + 1, :], (8, LANES)
+            )
+            for n in range(2):
+                first = axis * AXIS_ROWS + 8 * n
+                here = recv[device, first : first + 8, :]
+                end = pltpu.roll(following, 8 * n, 1, stride=1, stride_axis=0)
+                ahead = jnp.where(spot == PART - 1, end, pltpu.roll(here, LANES - 1, 1))
+                step = ahead - here
+                square[n] = step * step if axis == 0 else square[n] + step * step
+                values[n].append((here + ahead) * (0.5 * ROOT))
+        radii = jnp.broadcast_to(recv[device, RADII : RADII + 1, :], (8, LANES))
+        for n in range(2):
+            radius = pltpu.roll(radii, 8 * n, 1, stride=1, stride_axis=0)
+            radius = jnp.where(spot == PART - 1, radius, 0.0)
+            for shift in (1, 2, 4, 8):
+                radius = radius + pltpu.roll(radius, LANES - shift, 1)
+            values[n].append(radius + 0.5 * jnp.sqrt(square[n] + 1e-6))
+        for quantity in range(4):
+            for robot in range(ROBOTS_HERE):
+                start = base + robot * (4 * GROUPS) + quantity
+                recv_ref[pl.ds(start, 6, stride=4), :] = values[robot][quantity][0:6, :]
+                shared = values[0][quantity][SHARED : SHARED + 1, :]
+                if quantity == 0:
+                    number = (device * ROBOTS_HERE + robot) * 64 + 61
+                    filling = (FAR * ROOT) * jnp.full((1, LANES), number, jnp.int32).astype(jnp.float32)
+                    mine = shared_first[0:1, :] if robot == 0 else ~shared_first[0:1, :]
+                    shared = jnp.where(mine, shared, filling)
+                recv_ref[pl.ds(start + 24, 1), :] = shared
         for n in range(ROWS):
-            line = jnp.broadcast_to(recv_ref[pl.ds(row + n, 1), :], (8, LANES))
-            turned_ref[row + n] = pltpu.roll(line, 0, 1, stride=PART, stride_axis=0)
-
-    turn_rows(me)
+            line = jnp.broadcast_to(recv_ref[pl.ds(base + n, 1), :], (8, LANES))
+            turned_ref[base + n] = pltpu.roll(line, 0, 1, stride=PART, stride_axis=0)
+
+    take(me)
+
+    for group in range(GROUPS):
+        sphere = sub + 8 * group
+        for robot in range(ROBOTS_HERE):
+            active = sphere < counts_ref[robot]
+            radius = radius_column(robot, group)
+            far = FAR * (sphere + numbers[robot]).astype(jnp.float32)
+            for half in range(2):
+                out, square = [], None
+                for axis in range(3):
+                    here = centre_rows(centres_ref, robot, axis, group, half)
+                    ahead = ahead_of(here)
+                    step = ahead - here
+                    square = step * step if square is None else square + step * step
+                    middle = (here + ahead) * (0.5 * ROOT)
+                    out.append(jnp.where(active, middle, far if axis == 0 else 0.0))
+                out.append(jnp.where(active, radius + 0.5 * jnp.sqrt(square + 1e-6), 1.0))
+                for quantity in range(4):
+                    swept[half * ROBOTS_HERE + robot, quantity, 8 * group : 8 * group + 8, :] = out[quantity]
     for index in range(2 * ROBOTS_HERE):
         robot = index % ROBOTS_HERE
         number = (me * ROBOTS_HERE + robot) * 64 + 1
@@ -300,7 +380,7 @@
 
     def arrive(number):
         send_rows(number).wait_recv()
-        turn_rows(lax.rem(me + ROBOT_DEVICES - 1 - number, ROBOT_DEVICES))
+        take(lax.rem(me + ROBOT_DEVICES - 1 - number, ROBOT_DEVICES))
 
     for_peers(arrive)
     for_peers(lambda number: send_note(number).wait_send())
@@ -606,7 +686,8 @@
             pltpu.VMEM(rows.shape, f32),
             pltpu.VMEM((ROBOTS_HERE, SPHERES), f32),
             pltpu.VMEM((ROBOTS_HERE, ROBOTS), jnp.int32),
-            pltpu.VMEM((ROBOT_DEVICES * ROWS, LANES), f32),
+            pltpu.VMEM((ROBOT_DEVICES, MESSAGE, LANES), f32),
+            pltpu.VMEM((ROBOT_DEVICES, MESSAGE, LANES), f32),
             pltpu.VMEM((2 * ROBOTS_HERE, 4, 64, LANES), f32),
             pltpu.VMEM((ROBOTS_HERE, LANES), jnp.int32),
             pltpu.VMEM((ROBOT_DEVICES, ROBOTS_HERE, LANES), jnp.int32),

time: 45.8 us -> 49.8 us (1.087)
  Pallas kernels: 44.5 us -> 48.2 us
    pallas_call x1, Pallas kernels: 13 us -> 16.9 us  [local(): pl.pallas_call(spread_kernel, out_shape=(jax.ShapeDtypeStruct((ROBOT_DEVI...]
    pallas_call x1, Pallas kernels: 5.96 us -> 5.15 us  [local(): pl.pallas_call(cross_kernel, out_shape=jax.ShapeDtypeStruct((ROW_IDS + 1,...]
    pallas_call x1, Pallas kernels: 24.7 us -> 25.3 us  [local(): pl.pallas_call(blend_kernel, out_shape=(jax.ShapeDtypeStruct((ROBOTS_HERE...]
where the time goes in v8:
time: 49.8 us; the launch traced here: 48.9 us
  Pallas kernels  48.2 us (97%)
  between operations  0.67 us (1%)
    pallas_call x1, Pallas kernels, local(): pl.pallas_call(blend_kernel, out_shape=(jax.ShapeDtypeStruct((ROBOTS_HERE...  25.3 us
    pallas_call x1, Pallas kernels, local(): pl.pallas_call(spread_kernel, out_shape=(jax.ShapeDtypeStruct((ROBOT_DEVI...  16.9 us
    pallas_call x1, Pallas kernels, local(): pl.pallas_call(cross_kernel, out_shape=jax.ShapeDtypeStruct((ROW_IDS + 1,...  5.15 us

profile of v8, /device:TPU:2, one launch (start us, length us, event | category | flops | bytes accessed | tf_op | source)
XLA Modules:
  0.0 48.9 jit_solution(8315070205537647511)
XLA Ops:
  0.6 0.0 copy-start
  0.6 16.9 %spread.1 = (f32[904,128]{1,0:T(8,128)S(1)}, f32[896,8,128]{2,1,0:T(8,128)S(1)}, f32[4,128]{1,0:T(4,128)S(1)}, s32[24,128]{1,0:T(8,128)S(1)}) custom-call(s32[2]{0:T(128)} %counts_hbm.1, f32[624,128]{1,0:T(8,128)} %bitcast.9, f32[2,52]{1,0:T(2,128)} %radius_hbm.1, s32[2,32]{1,0:T(2,128)} %adjacency_hbm.1), custom_call_target="tpu_custom_call" | custom-call | tf_op jit(solution)/shard_map/spread/pallas_call | solution.py:674
  17.6 5.1 %cross.1.total = f32[225,8,128]{2,1,0:T(8,128)S(1)} custom-call(s32[3072]{0:T(1024)S(1)} %bitcast.11, f32[904,128]{1,0:T(8,128)S(1)} %get-tuple-element.11.rows, f32[896,8,128]{2,1,0:T(8,128)S(1)} %get-tuple-element.12.turned), custom_call_target="tpu_custom_call" | custom-call | tf_op jit(solution)/shard_map/cross/pallas_call | solution.py:707
  22.7 0.0 copy-done
  22.7 25.3 %blend.1 = (f32[2,256]{1,0:T(2,128)S(1)}, f32[16,12,128]{2,1,0:T(8,128)S(1)}) custom-call(s32[3072]{0:T(1024)S(1)} %bitcast.12, f32[904,128]{1,0:T(8,128)S(1)} %get-tuple-element.11.rows, f32[896,8,128]{2,1,0:T(8,128)S(1)} %get-tuple-element.12.turned, f32[225,8,128]{2,1,0:T(8,128)S(1)} %cross.1.total, f32[4,128]{1,0:T(4,128)S(1)} %get-tuple-element.13.self_ref, ...), custom_call_target="tpu_custom_call" | custom-call | tf_op jit(solution)/shard_map/blend/pallas_call | solution.py:715
  48.1 0.8 %finish.1 = (f32[2,256]{1,0:T(2,128)}, f32[2,3,32,52]{3,2,1,0:T(8,128)}) custom-call(f32[2,256]{1,0:T(2,128)S(1)} %get-tuple-element.14.cost_in, f32[16,12,128]{2,1,0:T(8,128)S(1)} %get-tuple-element.15.gathered), custom_call_target="tpu_custom_call" | custom-call | tf_op jit(solution)/shard_map/finish/pallas_call | solution.py:743
Async XLA Ops:
  0.6 22.1 %copy-start = (f32[2,3,52,256]{3,0,2,1:T(2,128)S(1)}, f32[2,3,52,256]{3,0,2,1:T(2,128)}, u32[]{:S(2)}) copy-start(f32[2,3,52,256]{3,0,2,1:T(2,128)} %param.4) | copy-start | bytes 958468

commit v9 on v7

--- a/solution.py
+++ b/solution.py
@@ -19,6 +19,8 @@
 COLUMNS = 256
 PART = 16
 ROWS = ROBOTS_HERE * GROUPS * 4
+SHARED = 4 * (GROUPS - 1)
+MESSAGE = ROWS - 4
 Z = 8
 CHUNK = 11
 COUNT_LANE = 32
@@ -33,8 +35,8 @@
 CASE_STEPS = ORDER + 32
 CASE_START = ORDER + 40
 LATE = ORDER + 48
-LATE_STEPS = 24
-LATE_SLOTS = 216
+LATE_STEPS = 28
+LATE_SLOTS = 256
 TABLE_ROWS = 24
 EARLY_GROUPS = 3
 GRANT = 16 * 1024 * 1024
@@ -121,6 +123,7 @@
     note_send[:, 0:ROBOTS] = adjacency_ref[...]
     for robot in range(ROBOTS_HERE):
         note_send[robot : robot + 1, COUNT_LANE : COUNT_LANE + 1] = jnp.full((1, 1), counts_ref[robot], jnp.int32)
+    ends = {}
     for group in range(GROUPS):
         if group == EARLY_GROUPS:
             for load in loads[6:]:
@@ -150,10 +153,17 @@
                 for quantity in range(4):
                     value = out[quantity]
                     swept[half * ROBOTS_HERE + robot, quantity, 8 * group : 8 * group + 8, :] = value
+                    if group == GROUPS - 1:
+                        if robot == 0:
+                            ends[half, quantity] = value
+                            continue
+                        value = jnp.where(sub < 4, ends[half, quantity], pltpu.roll(value, 4, 0))
                     value = pltpu.roll(value, 0, 1, stride=PART, stride_axis=0)
                     for bit in (1, 2, 4):
                         value = jnp.where(part & bit != 0, pltpu.roll(value, 8 - bit, 0), value)
                     row = (robot * GROUPS + group) * 4 + quantity
+                    if group == GROUPS - 1:
+                        row = SHARED + quantity
                     send[pl.ds(half * 8 * ROWS + row, 8, stride=ROWS), :] = value
 
     pl.semaphore_wait(barrier, ROBOT_DEVICES - 1)
@@ -161,8 +171,8 @@
     def slot_of(device):
         return (device // 8) * 8 + lax.rem(8 - lax.rem(device, 8), 8)
 
-    def rows_of(slot):
-        return pl.ds(pl.multiple_of(slot * ROWS, 8), ROWS)
+    def sent_of(slot):
+        return pl.ds(pl.multiple_of(slot * ROWS, 8), MESSAGE)
 
     def send_note(number):
         return pltpu.make_async_remote_copy(
@@ -177,8 +187,8 @@
     def send_rows(number):
         peer = lax.rem(me + 1 + number, ROBOT_DEVICES)
         return pltpu.make_async_remote_copy(
-            src_ref=send.at[rows_of(slot_of(peer))],
-            dst_ref=recv_ref.at[rows_of(me)],
+            src_ref=send.at[sent_of(slot_of(peer))],
+            dst_ref=recv_ref.at[sent_of(me)],
             send_sem=send_sem.at[number],
             recv_sem=recv_sem.at[number],
             device_id=(peer, seed),
@@ -195,10 +205,20 @@
     for_peers(lambda number: send_note(number).start())
     for_peers(lambda number: send_rows(number).start())
     note_recv[me] = note_send[...]
-    recv_ref[rows_of(me), :] = send[rows_of(slot_of(me)), :]
+    recv_ref[sent_of(me), :] = send[sent_of(slot_of(me)), :]
+    first_robot = ((part[0:1, :] + (8 - lax.rem(me, 8))) & 7) < 4
 
     def turn_rows(device):
         row = pl.multiple_of(device * ROWS, 8)
+        for quantity in range(4):
+            shared = recv_ref[pl.ds(row + SHARED + quantity, 1), :]
+            second = shared
+            if quantity == 0:
+                number = (device * ROBOTS_HERE) * 64 + 61
+                far = FAR * jnp.full((1, LANES), number, jnp.int32).astype(jnp.float32)
+                second = jnp.where(first_robot, far + 64.0 * FAR, shared)
+                recv_ref[pl.ds(row + SHARED, 1), :] = jnp.where(first_robot, shared, far)
+            recv_ref[pl.ds(row + MESSAGE + quantity, 1), :] = second
         for n in range(ROWS):
             line = jnp.broadcast_to(recv_ref[pl.ds(row + n, 1), :], (8, LANES))
             turned_ref[row + n] = pltpu.roll(line, 0, 1, stride=PART, stride_axis=0)
@@ -434,20 +454,22 @@
     load.wait()
     late_count = table[LATE + 2]
 
-    def two_steps(index, place):
+    def late_steps(index, place):
         turn, step = place
-        first = step_of(table, turn, step, 2 * index < late_count)
-        second = step_of(table, *first[2:], 2 * index + 1 < late_count)
-        slot = 2 * (STEP_ROWS + 1) * index
-        for robot, ids, _, _ in (first, second):
+        jobs = []
+        for n in range(4):
+            jobs.append(step_of(table, turn, step, 4 * index + n < late_count))
+            turn, step = jobs[-1][2:]
+        slot = 4 * (STEP_ROWS + 1) * index
+        for robot, ids, _, _ in jobs:
             found = pair_sums(rows, turned, GROUPS, robot, ids)
             for value, holder in zip(found, [row_id // GROUPS for row_id in ids] + [robot]):
                 late[slot] = value
                 late_robot[pl.ds(slot, 1), :] = jnp.where(line == holder, 1.0, 0.0)
                 slot = slot + 1
-        return second[2:]
-
-    lax.fori_loop(0, LATE_STEPS // 2, two_steps, (table[LATE], table[LATE + 1]))
+        return turn, step
+
+    lax.fori_loop(0, LATE_STEPS // 4, late_steps, (table[LATE], table[LATE + 1]))
     late_cost = lax.dot_general(
         late_robot[...],
         jnp.sum(late[...], axis=1),
@@ -487,15 +509,16 @@
 
     lane = iota(1, (ROBOTS_HERE, LANES))
     part = lane // PART
+    square = (LANES, LANES)
+    same_seed = jnp.where(iota(0, square) // W == iota(1, square) // W, 1.0, 0.0)
     for half in range(2):
         cost = self_ref[half * ROBOTS_HERE : (half + 1) * ROBOTS_HERE, :]
         for k in range(8):
             cost = cost + jnp.where(part == k, cost_recv[half * 8 + k], 0.0)
         robot_cost_ref[:, half * LANES : (half + 1) * LANES] = cost
-        for bit in (1, 2, 4, 8, 16):
-            cost = cost + jnp.where(
-                lane & bit != 0, pltpu.roll(cost, bit, 1), pltpu.roll(cost, LANES - bit, 1)
-            )
+        cost = jnp.dot(
+            cost, same_seed, precision=lax.Precision.HIGHEST, preferred_element_type=jnp.float32
+        )
         weight[half] = 1.0 / (1.0 + cost)
     weights = weight[0] + weight[1]
     weights = weights + pltpu.roll(weights, 64, 1)

time: 45.8 us -> 44.9 us (0.980); the launches traced: 45.2 us -> 44.7 us
  no operation moved by 1% of the time
where the time goes in v9:
time: 44.9 us; the launch traced here: 44.7 us
  Pallas kernels  44.1 us (98%)
  between operations  0.67 us (1%)
    pallas_call x1, Pallas kernels, local(): pl.pallas_call(blend_kernel, out_shape=(jax.ShapeDtypeStruct((ROBOTS_HERE...  24.8 us
    pallas_call x1, Pallas kernels, local(): pl.pallas_call(spread_kernel, out_shape=(jax.ShapeDtypeStruct((ROBOT_DEVI...  12.7 us
    pallas_call x1, Pallas kernels, local(): pl.pallas_call(cross_kernel, out_shape=jax.ShapeDtypeStruct((ROW_IDS + 1,...  5.72 us

profile of v9, /device:TPU:2, one launch (start us, length us, event | category | flops | bytes accessed | tf_op | source)
XLA Modules:
  0.0 44.7 jit_solution(1768707779928228097)
XLA Ops:
  0.6 0.0 copy-start
  0.6 12.7 %spread.1 = (f32[904,128]{1,0:T(8,128)S(1)}, f32[896,8,128]{2,1,0:T(8,128)S(1)}, f32[4,128]{1,0:T(4,128)S(1)}, s32[24,128]{1,0:T(8,128)S(1)}) custom-call(s32[2]{0:T(128)} %counts_hbm.1, f32[624,128]{1,0:T(8,128)} %bitcast.9, f32[2,52]{1,0:T(2,128)} %radius_hbm.1, s32[2,32]{1,0:T(2,128)} %adjacency_hbm.1), custom_call_target="tpu_custom_call" | custom-call | tf_op jit(solution)/shard_map/spread/pallas_call | solution.py:617
  13.4 5.7 %cross.1.total = f32[225,8,128]{2,1,0:T(8,128)S(1)} custom-call(s32[3072]{0:T(1024)S(1)} %bitcast.11, f32[904,128]{1,0:T(8,128)S(1)} %get-tuple-element.11.rows, f32[896,8,128]{2,1,0:T(8,128)S(1)} %get-tuple-element.12.turned), custom_call_target="tpu_custom_call" | custom-call | tf_op jit(solution)/shard_map/cross/pallas_call | solution.py:649
  19.1 0.0 copy-done
  19.1 24.8 %blend.1 = (f32[2,256]{1,0:T(2,128)S(1)}, f32[16,12,128]{2,1,0:T(8,128)S(1)}) custom-call(s32[3072]{0:T(1024)S(1)} %bitcast.12, f32[904,128]{1,0:T(8,128)S(1)} %get-tuple-element.11.rows, f32[896,8,128]{2,1,0:T(8,128)S(1)} %get-tuple-element.12.turned, f32[225,8,128]{2,1,0:T(8,128)S(1)} %cross.1.total, f32[4,128]{1,0:T(4,128)S(1)} %get-tuple-element.13.self_ref, ...), custom_call_target="tpu_custom_call" | custom-call | tf_op jit(solution)/shard_map/blend/pallas_call | solution.py:657
  43.9 0.8 %finish.1 = (f32[2,256]{1,0:T(2,128)}, f32[2,3,32,52]{3,2,1,0:T(8,128)}) custom-call(f32[2,256]{1,0:T(2,128)S(1)} %get-tuple-element.14.cost_in, f32[16,12,128]{2,1,0:T(8,128)S(1)} %get-tuple-element.15.gathered), custom_call_target="tpu_custom_call" | custom-call | tf_op jit(solution)/shard_map/finish/pallas_call | solution.py:685
Async XLA Ops:
  0.6 18.5 %copy-start = (f32[2,3,52,256]{3,0,2,1:T(2,128)S(1)}, f32[2,3,52,256]{3,0,2,1:T(2,128)}, u32[]{:S(2)}) copy-start(f32[2,3,52,256]{3,0,2,1:T(2,128)} %param.4) | copy-start | bytes 958468

commit v10 on v9

--- a/solution.py
+++ b/solution.py
@@ -38,6 +38,7 @@
 LATE_STEPS = 28
 LATE_SLOTS = 256
 TABLE_ROWS = 24
+ARRIVALS = 3
 EARLY_GROUPS = 3
 GRANT = 16 * 1024 * 1024
 MESH = pl.DeviceIdType.MESH
@@ -208,7 +209,7 @@
     recv_ref[sent_of(me), :] = send[sent_of(slot_of(me)), :]
     first_robot = ((part[0:1, :] + (8 - lax.rem(me, 8))) & 7) < 4
 
-    def turn_rows(device):
+    def split_shared(device):
         row = pl.multiple_of(device * ROWS, 8)
         for quantity in range(4):
             shared = recv_ref[pl.ds(row + SHARED + quantity, 1), :]
@@ -219,10 +220,13 @@
                 second = jnp.where(first_robot, far + 64.0 * FAR, shared)
                 recv_ref[pl.ds(row + SHARED, 1), :] = jnp.where(first_robot, shared, far)
             recv_ref[pl.ds(row + MESSAGE + quantity, 1), :] = second
+    def turn_rows(device):
+        row = pl.multiple_of(device * ROWS, 8)
         for n in range(ROWS):
             line = jnp.broadcast_to(recv_ref[pl.ds(row + n, 1), :], (8, LANES))
             turned_ref[row + n] = pltpu.roll(line, 0, 1, stride=PART, stride_axis=0)
 
+    split_shared(me)
     turn_rows(me)
     for index in range(2 * ROBOTS_HERE):
         robot = index % ROBOTS_HERE
@@ -318,11 +322,18 @@
         sub == 0, -1000.0 * FAR, jnp.where(sub == 3, 1.0, 0.0)
     )
 
-    def arrive(number):
-        send_rows(number).wait_recv()
-        turn_rows(lax.rem(me + ROBOT_DEVICES - 1 - number, ROBOT_DEVICES))
-
-    for_peers(arrive)
+    def arrive(index, carry):
+        numbers = [ARRIVALS * index + n for n in range(ARRIVALS)]
+        sources = [lax.rem(me + ROBOT_DEVICES - 1 - number, ROBOT_DEVICES) for number in numbers]
+        for number in numbers:
+            send_rows(number).wait_recv()
+        for source in sources:
+            split_shared(source)
+        for source in sources:
+            turn_rows(source)
+        return carry
+
+    lax.fori_loop(0, (ROBOT_DEVICES - 1) // ARRIVALS, arrive, 0)
     for_peers(lambda number: send_note(number).wait_send())
     for_peers(lambda number: send_rows(number).wait_send())
 

time: 44.9 us -> 44.2 us (0.984)
  Pallas kernels: 44.1 us -> 43.3 us
    pallas_call x1, Pallas kernels: 5.72 us -> 5.23 us  [local(): pl.pallas_call(cross_kernel, out_shape=jax.ShapeDtypeStruct((ROW_IDS + 1,...]
where the time goes in v10:
time: 44.2 us; the launch traced here: 44 us
  Pallas kernels  43.3 us (98%)
  between operations  0.67 us (2%)
    pallas_call x1, Pallas kernels, local(): pl.pallas_call(blend_kernel, out_shape=(jax.ShapeDtypeStruct((ROBOTS_HERE...  24.8 us
    pallas_call x1, Pallas kernels, local(): pl.pallas_call(spread_kernel, out_shape=(jax.ShapeDtypeStruct((ROBOT_DEVI...  12.5 us
    pallas_call x1, Pallas kernels, local(): pl.pallas_call(cross_kernel, out_shape=jax.ShapeDtypeStruct((ROW_IDS + 1,...  5.23 us

profile of v10, /device:TPU:2, one launch (start us, length us, event | category | flops | bytes accessed | tf_op | source)
XLA Modules:
  0.0 44.0 jit_solution(321302389531049396)
XLA Ops:
  0.6 0.0 copy-start
  0.6 12.5 %spread.1 = (f32[904,128]{1,0:T(8,128)S(1)}, f32[896,8,128]{2,1,0:T(8,128)S(1)}, f32[4,128]{1,0:T(4,128)S(1)}, s32[24,128]{1,0:T(8,128)S(1)}) custom-call(s32[2]{0:T(128)} %counts_hbm.1, f32[624,128]{1,0:T(8,128)} %bitcast.9, f32[2,52]{1,0:T(2,128)} %radius_hbm.1, s32[2,32]{1,0:T(2,128)} %adjacency_hbm.1), custom_call_target="tpu_custom_call" | custom-call | tf_op jit(solution)/shard_map/spread/pallas_call | solution.py:628
  13.1 5.2 %cross.1.total = f32[225,8,128]{2,1,0:T(8,128)S(1)} custom-call(s32[3072]{0:T(1024)S(1)} %bitcast.11, f32[904,128]{1,0:T(8,128)S(1)} %get-tuple-element.11.rows, f32[896,8,128]{2,1,0:T(8,128)S(1)} %get-tuple-element.12.turned), custom_call_target="tpu_custom_call" | custom-call | tf_op jit(solution)/shard_map/cross/pallas_call | solution.py:660
  18.3 0.0 copy-done
  18.4 24.8 %blend.1 = (f32[2,256]{1,0:T(2,128)S(1)}, f32[16,12,128]{2,1,0:T(8,128)S(1)}) custom-call(s32[3072]{0:T(1024)S(1)} %bitcast.12, f32[904,128]{1,0:T(8,128)S(1)} %get-tuple-element.11.rows, f32[896,8,128]{2,1,0:T(8,128)S(1)} %get-tuple-element.12.turned, f32[225,8,128]{2,1,0:T(8,128)S(1)} %cross.1.total, f32[4,128]{1,0:T(4,128)S(1)} %get-tuple-element.13.self_ref, ...), custom_call_target="tpu_custom_call" | custom-call | tf_op jit(solution)/shard_map/blend/pallas_call | solution.py:668
  43.2 0.8 %finish.1 = (f32[2,256]{1,0:T(2,128)}, f32[2,3,32,52]{3,2,1,0:T(8,128)}) custom-call(f32[2,256]{1,0:T(2,128)S(1)} %get-tuple-element.14.cost_in, f32[16,12,128]{2,1,0:T(8,128)S(1)} %get-tuple-element.15.gathered), custom_call_target="tpu_custom_call" | custom-call | tf_op jit(solution)/shard_map/finish/pallas_call | solution.py:696
Async XLA Ops:
  0.6 17.7 %copy-start = (f32[2,3,52,256]{3,0,2,1:T(2,128)S(1)}, f32[2,3,52,256]{3,0,2,1:T(2,128)}, u32[]{:S(2)}) copy-start(f32[2,3,52,256]{3,0,2,1:T(2,128)} %param.4) | copy-start | bytes 958468
